TPU v7x, 512 devices: a whole 4x8x8 slice. The times are simulated.
512 devices in a mesh: grp: 16 (over y, x_lo), row: 8 (over z), col: 4 (over x_hi, core).
Axes of the slice: x: 4 (x_hi: 2, x_lo: 2; x = x_hi * 2 + x_lo), y: 8, z: 8, core: 2. Of those that a mesh axis runs over, the one named last changes fastest.
Arguments:
- normals: float32 [16, 4096, 4096], P('grp', 'row', 'col'), as said below
- transforms: float32 [16, 32, 128, 128], P('grp', 'row'), as said below
- block_map: int32 [16, 32], P('grp'), may hold values from 0 to 31, as said below
Outputs:
- eliminated: float32 [4096, 4096], P('row', 'col')
Inputs may be any that keep to these rules, and one draw needn't show every extreme that they name: `block_map`: for each group, a permutation of the blocks that maps every aligned range of 4 blocks onto itself. `normals`: each group's matrix is symmetric positive definite. `transforms`: each block is nonsingular.
All inputs are finite; a program needn't handle non-finite values.
Results may differ from a plain program's by a relative error of at most 0.0001.
Values sent between devices are 32-bit elements; how exact they have to be, the bound alone decides.
A program may use at most 64 MiB of HBM per device.

v0:
```python
import jax
import jax.numpy as jnp
from jax import lax
from jax.sharding import PartitionSpec as P

BLK = 128
NPAN = 5


def split_up(shard, dim, length):
    shape = shard.shape
    parts = shard.reshape(*shape[:dim], length, shape[dim] // length, *shape[dim + 1 :])
    return jnp.moveaxis(parts, dim, 0)


def sum_at_owner(shard, axis, dim):
    parts = split_up(shard, dim, lax.axis_size(axis))
    arrived = lax.all_to_all(parts, axis, split_axis=0, concat_axis=0, tiled=True)
    return arrived.sum(axis=0)


def from_root(shard, axis, root):
    return lax.dynamic_index_in_dim(lax.all_gather(shard, axis), root, 0, keepdims=False)


def in_order(parts, dim):
    parts = jnp.moveaxis(parts, 0, dim)
    shape = parts.shape
    return parts.reshape(*shape[:dim], shape[dim] * shape[dim + 1], *shape[dim + 2 :])


def sent_to_all(shard, axis):
    length = lax.axis_size(axis)
    return lax.all_to_all(
        jnp.broadcast_to(shard[None], (length, *shard.shape)), axis, 0, 0, tiled=True
    )


def gather_directly(shard, axis, dim):
    return in_order(sent_to_all(shard, axis), dim)


def on_device(normals, transforms, block_map):
    local = normals[0]
    height, width = local.shape
    row_blocks = height // BLK
    col_blocks = width // BLK
    row_index = lax.axis_index("row")
    col_index = lax.axis_index("col")
    row_transforms = transforms[0]
    every_block = lax.all_gather(transforms, "row", axis=1, tiled=True)[0]
    col_transforms = lax.dynamic_slice_in_dim(every_block, col_index * col_blocks, col_blocks, 0)
    grid = local.reshape(row_blocks, BLK, col_blocks, BLK)
    half_done = jnp.einsum("aij,aibk->ajbk", row_transforms, grid, precision=lax.Precision.HIGHEST)
    rotated = jnp.einsum(
        "ajbk,bkl->ajbl", half_done, col_transforms, precision=lax.Precision.HIGHEST
    )
    mapping = block_map[0]
    row_map = (
        lax.dynamic_slice_in_dim(mapping, row_index * row_blocks, row_blocks, 0)
        - row_index * row_blocks
    )
    col_map = (
        lax.dynamic_slice_in_dim(mapping, col_index * col_blocks, col_blocks, 0)
        - col_index * col_blocks
    )
    rotated = jnp.take(rotated, row_map, axis=0)
    rotated = jnp.take(rotated, col_map, axis=2).reshape(height, width)
    matrix = sum_at_owner(rotated, "grp", 0)
    row_offset = row_index * height + lax.axis_index("grp") * matrix.shape[0]
    own_count = matrix.shape[0]
    order_all = height * lax.axis_size("row")
    col_offset = col_index * width
    for panel in range(NPAN):
        offset = panel * BLK
        holder = offset // width
        inside = offset - holder * width
        panel_piece = from_root(matrix[:, inside : inside + BLK], "col", holder)
        panel_piece = gather_directly(panel_piece, "grp", 0)
        column = lax.all_gather(panel_piece, "row", axis=0, tiled=True)
        factor_block = jnp.linalg.cholesky(column[offset : offset + BLK])
        factor = lax.linalg.triangular_solve(
            factor_block, column, left_side=False, lower=True, transpose_a=True
        )
        below = jnp.arange(order_all)[:, None] >= offset
        factor = jnp.where(below, factor, jnp.zeros_like(factor))
        own_rows = lax.dynamic_slice_in_dim(factor, row_offset, own_count, 0)
        col_rows = lax.dynamic_slice_in_dim(factor, col_offset, width, 0)
        matrix = matrix - jnp.dot(
            own_rows,
            col_rows.T,
            precision=lax.Precision.HIGHEST,
            preferred_element_type=jnp.float32,
        )
        current = matrix[:, inside : inside + BLK]
        matrix = matrix.at[:, inside : inside + BLK].set(
            jnp.where(col_index == holder, own_rows, current)
        )
    matrix = gather_directly(matrix, "grp", 0)
    return matrix


def solution(mesh):
    return jax.shard_map(
        on_device,
        mesh=mesh,
        in_specs=(P("grp", "row", "col"), P("grp", "row", None, None), P("grp", None)),
        out_specs=P("row", "col"),
        check_vma=False,
    )
```

profile of v0, /device:TPU:1, one launch (start us, length us, event | category | flops | bytes accessed | tf_op | source)
XLA Modules:
  0.0 664.4 jit_solution(9049926611283162796)
XLA Ops:
  6.5 0.7 all-gather.12.cloned.1.call-update
  7.3 3.4 copy.93
  11.2 3.7 fusion.4
  14.9 39.9 %all-gather.12.cloned.1.call-done = f32[1,32,128,128]{3,2,0,1:T(8,128)} async-done(((f32[1,4,128,128]{3,2,0,1:T(8,128)}), f32[1,32,128,128]{3,2,0,1:T(8,128)}) %all-gather.12.cloned.1.call-update) | async-done | bytes 2097168 | tf_op jit(solution)/shard_map/all_gather | solution.py:51
  54.8 4.3 convolution_bitcast_fusion.5
  59.1 2.3 gather_fusion
  61.4 1.6 broadcast_select_fusion.1
  63.0 2.3 gather_fusion.1
  65.3 1.8 copy.69
  67.1 1.7 gather.12
  69.0 53.1 %all_to_all.35 = f32[16,32,1024]{2,1,0:T(8,128)S(1)} all-to-all(f32[16,32,1024]{2,1,0:T(8,128)S(1)} %broadcast_select_fusion), channel_id=1, replica_groups=mesh['grp'=16,'row'=8,'col'=4] {'grp'}, dimensions={0} | all-to-all | bytes 4194304 | tf_op jit(solution)/shard_map/all_to_all | solution.py:18
  122.3 12.6 %all-gather = f32[128,128]{1,0:T(8,128)S(1)} all-gather(f32[32,128]{1,0:T(8,128)S(1)} %slice.165), channel_id=2, replica_groups=mesh['grp'=16,'row'=8,'col'=4] {'col'}, dimensions={0}, use_global_device_ids=true | all-gather | bytes 81920 | tf_op jit(solution)/shard_map/all_gather | solution.py:23
  134.9 13.9 %all_to_all.36 = f32[16,32,128]{2,1,0:T(8,128)S(1)} all-to-all(f32[16,32,128]{2,1,0:T(8,128)S(1)} %broadcast_in_dim.111), channel_id=1, replica_groups=mesh['grp'=16,'row'=8,'col'=4] {'grp'}, dimensions={0} | all-to-all | bytes 524288 | tf_op jit(solution)/shard_map/all_to_all | solution.py:34
  148.8 0.8 copy.70
  150.6 33.5 %all-gather.14.cloned.1.call-done = f32[4096,128]{0,1:T(8,128)} async-done(((f32[512,128]{0,1:T(8,128)}), f32[4096,128]{0,1:T(8,128)}) %all-gather.14.cloned.1.call-update) | async-done | bytes 2097168 | tf_op jit(solution)/shard_map/all_gather | solution.py:80
  184.1 0.8 slice.167
  185.0 0.9 fusion.28
  185.9 11.7 %cholesky.89 = f32[128,128]{1,0:T(8,128)S(1)} custom-call(f32[128,128]{1,0:T(8,128)S(1)} %fusion.28), custom_call_target="Cholesky" | custom-call | tf_op jit(solution)/shard_map/jit(cholesky)/cholesky | solution.py:81
  198.2 0.7 fusion.14
  198.9 9.8 %custom-call.9 = f32[1,128,128]{1,2,0:T(8,128)S(1)} custom-call(f32[1,128,128]{2,1,0:T(8,128)S(1)} %fusion.14), custom_call_target="InvertDiagBlocksLowerTriangular" | custom-call | tf_op jit(solution)/shard_map/triangular_solve/custom-call.0 | solution.py:82
  208.7 5.1 convolution_bitcast_fusion.4
  215.1 11.4 %all-gather.1 = f32[128,128]{1,0:T(8,128)S(1)} all-gather(f32[32,128]{1,0:T(8,128)S(1)} %slice.169), channel_id=3, replica_groups=mesh['grp'=16,'row'=8,'col'=4] {'col'}, dimensions={0}, use_global_device_ids=true | all-gather | bytes 81920 | tf_op jit(solution)/shard_map/all_gather | solution.py:23
  226.5 18.6 %all_to_all.37 = f32[16,32,128]{2,1,0:T(8,128)S(1)} all-to-all(f32[16,32,128]{2,1,0:T(8,128)S(1)} %broadcast_in_dim.114), channel_id=1, replica_groups=mesh['grp'=16,'row'=8,'col'=4] {'grp'}, dimensions={0} | all-to-all | bytes 524288 | tf_op jit(solution)/shard_map/all_to_all | solution.py:34
  245.1 0.8 copy.73
  246.2 0.6 compare_reduce_fusion.8
  246.9 33.8 %all-gather.16.cloned.1.call-done = f32[4096,128]{0,1:T(8,128)} async-done(((f32[512,128]{0,1:T(8,128)}), f32[4096,128]{0,1:T(8,128)}) %all-gather.16.cloned.1.call-update) | async-done | bytes 2097168 | tf_op jit(solution)/shard_map/all_gather | solution.py:80
  280.7 0.8 slice.171
  281.6 0.9 fusion.26
  282.5 11.7 %cholesky.100 = f32[128,128]{1,0:T(8,128)S(1)} custom-call(f32[128,128]{1,0:T(8,128)S(1)} %fusion.26), custom_call_target="Cholesky" | custom-call | tf_op jit(solution)/shard_map/jit(cholesky)/cholesky | solution.py:81
  294.9 0.7 fusion.15
  295.5 9.8 %custom-call.10 = f32[1,128,128]{1,2,0:T(8,128)S(1)} custom-call(f32[1,128,128]{2,1,0:T(8,128)S(1)} %fusion.15), custom_call_target="InvertDiagBlocksLowerTriangular" | custom-call | tf_op jit(solution)/shard_map/triangular_solve/custom-call.0 | solution.py:82
  305.4 5.3 fusion.3
  311.9 11.4 %all-gather.2 = f32[128,128]{1,0:T(8,128)S(1)} all-gather(f32[32,128]{1,0:T(8,128)S(1)} %slice.173), channel_id=4, replica_groups=mesh['grp'=16,'row'=8,'col'=4] {'col'}, dimensions={0}, use_global_device_ids=true | all-gather | bytes 81920 | tf_op jit(solution)/shard_map/all_gather | solution.py:23
  323.3 18.6 %all_to_all.38 = f32[16,32,128]{2,1,0:T(8,128)S(1)} all-to-all(f32[16,32,128]{2,1,0:T(8,128)S(1)} %broadcast_in_dim.117), channel_id=1, replica_groups=mesh['grp'=16,'row'=8,'col'=4] {'grp'}, dimensions={0} | all-to-all | bytes 524288 | tf_op jit(solution)/shard_map/all_to_all | solution.py:34
  341.9 0.8 copy.76
  343.9 33.6 %all-gather.18.cloned.1.call-done = f32[4096,128]{0,1:T(8,128)} async-done(((f32[512,128]{0,1:T(8,128)}), f32[4096,128]{0,1:T(8,128)}) %all-gather.18.cloned.1.call-update) | async-done | bytes 2097168 | tf_op jit(solution)/shard_map/all_gather | solution.py:80
  377.5 0.8 slice.175
  378.4 0.9 fusion.24
  379.3 11.7 %cholesky.111 = f32[128,128]{1,0:T(8,128)S(1)} custom-call(f32[128,128]{1,0:T(8,128)S(1)} %fusion.24), custom_call_target="Cholesky" | custom-call | tf_op jit(solution)/shard_map/jit(cholesky)/cholesky | solution.py:81
  391.7 0.7 fusion.16
  392.4 9.8 %custom-call.11 = f32[1,128,128]{1,2,0:T(8,128)S(1)} custom-call(f32[1,128,128]{2,1,0:T(8,128)S(1)} %fusion.16), custom_call_target="InvertDiagBlocksLowerTriangular" | custom-call | tf_op jit(solution)/shard_map/triangular_solve/custom-call.0 | solution.py:82
  402.2 5.3 fusion.2
  408.7 11.4 %all-gather.3 = f32[128,128]{1,0:T(8,128)S(1)} all-gather(f32[32,128]{1,0:T(8,128)S(1)} %slice.177), channel_id=5, replica_groups=mesh['grp'=16,'row'=8,'col'=4] {'col'}, dimensions={0}, use_global_device_ids=true | all-gather | bytes 81920 | tf_op jit(solution)/shard_map/all_gather | solution.py:23
  420.2 18.6 %all_to_all.39 = f32[16,32,128]{2,1,0:T(8,128)S(1)} all-to-all(f32[16,32,128]{2,1,0:T(8,128)S(1)} %broadcast_in_dim.120), channel_id=1, replica_groups=mesh['grp'=16,'row'=8,'col'=4] {'grp'}, dimensions={0} | all-to-all | bytes 524288 | tf_op jit(solution)/shard_map/all_to_all | solution.py:34
  438.7 0.8 copy.79
  440.5 33.9 %all-gather.20.cloned.1.call-done = f32[4096,128]{0,1:T(8,128)} async-done(((f32[512,128]{0,1:T(8,128)}), f32[4096,128]{0,1:T(8,128)}) %all-gather.20.cloned.1.call-update) | async-done | bytes 2097168 | tf_op jit(solution)/shard_map/all_gather | solution.py:80
  474.3 0.8 slice.179
  475.3 0.9 fusion.22
  476.1 11.7 %cholesky.122 = f32[128,128]{1,0:T(8,128)S(1)} custom-call(f32[128,128]{1,0:T(8,128)S(1)} %fusion.22), custom_call_target="Cholesky" | custom-call | tf_op jit(solution)/shard_map/jit(cholesky)/cholesky | solution.py:81
  488.5 0.7 fusion.17
  489.2 9.8 %custom-call.12 = f32[1,128,128]{1,2,0:T(8,128)S(1)} custom-call(f32[1,128,128]{2,1,0:T(8,128)S(1)} %fusion.17), custom_call_target="InvertDiagBlocksLowerTriangular" | custom-call | tf_op jit(solution)/shard_map/triangular_solve/custom-call.0 | solution.py:82
  499.0 5.3 fusion.1
  505.5 11.4 %all-gather.4 = f32[128,128]{1,0:T(8,128)S(1)} all-gather(f32[32,128]{1,0:T(8,128)S(1)} %slice.181), channel_id=6, replica_groups=mesh['grp'=16,'row'=8,'col'=4] {'col'}, dimensions={0}, use_global_device_ids=true | all-gather | bytes 81920 | tf_op jit(solution)/shard_map/all_gather | solution.py:23
  517.0 18.8 %all_to_all.40 = f32[16,32,128]{2,1,0:T(8,128)S(1)} all-to-all(f32[16,32,128]{2,1,0:T(8,128)S(1)} %broadcast_in_dim.123), channel_id=1, replica_groups=mesh['grp'=16,'row'=8,'col'=4] {'grp'}, dimensions={0} | all-to-all | bytes 524288 | tf_op jit(solution)/shard_map/all_to_all | solution.py:34
  535.7 0.8 copy.82
  537.3 34.1 %all-gather.22.cloned.1.call-done = f32[4096,128]{0,1:T(8,128)} async-done(((f32[512,128]{0,1:T(8,128)}), f32[4096,128]{0,1:T(8,128)}) %all-gather.22.cloned.1.call-update) | async-done | bytes 2097168 | tf_op jit(solution)/shard_map/all_gather | solution.py:80
  571.4 0.8 slice.183
  572.3 0.9 fusion.20
  573.2 11.7 %cholesky.133 = f32[128,128]{1,0:T(8,128)S(1)} custom-call(f32[128,128]{1,0:T(8,128)S(1)} %fusion.20), custom_call_target="Cholesky" | custom-call | tf_op jit(solution)/shard_map/jit(cholesky)/cholesky | solution.py:81
  585.6 0.7 fusion.18
  586.2 9.8 %custom-call.13 = f32[1,128,128]{1,2,0:T(8,128)S(1)} custom-call(f32[1,128,128]{2,1,0:T(8,128)S(1)} %fusion.18), custom_call_target="InvertDiagBlocksLowerTriangular" | custom-call | tf_op jit(solution)/shard_map/triangular_solve/custom-call.0 | solution.py:82
  596.0 5.3 fusion
  602.8 53.2 %all_to_all.41 = f32[16,32,1024]{2,1,0:T(8,128)S(1)} all-to-all(f32[16,32,1024]{2,1,0:T(8,128)S(1)} %broadcast_in_dim.125), channel_id=1, replica_groups=mesh['grp'=16,'row'=8,'col'=4] {'grp'}, dimensions={0} | all-to-all | bytes 4194304 | tf_op jit(solution)/shard_map/all_to_all | solution.py:34
  656.0 1.3 copy.102
  (73 shorter events, 15.0 us)
Async XLA Ops:
  6.5 48.3 %all-gather.12.cloned.1.call-start = ((), (), s32[]{:S(2)}) async-start(), calls=%async_computation.7 | async-start | bytes 2359296 | tf_op jit(solution)/shard_map/all_gather | solution.py:51
  7.3 176.8 %all-gather.14.cloned.1.call-start = ((), (), s32[]{:S(2)}) async-start(), calls=%async_computation.8 | async-start | bytes 2359296 | tf_op jit(solution)/shard_map/all_gather | solution.py:80
  7.3 3.4 copy-start.1
  7.3 3.8 copy-start
  149.7 131.0 %all-gather.16.cloned.1.call-start = ((), (), s32[]{:S(2)}) async-start(), calls=%async_computation.9 | async-start | bytes 2359296 | tf_op jit(solution)/shard_map/all_gather | solution.py:80
  246.0 131.5 %all-gather.18.cloned.1.call-start = ((), (), s32[]{:S(2)}) async-start(), calls=%async_computation.10 | async-start | bytes 2359296 | tf_op jit(solution)/shard_map/all_gather | solution.py:80
  342.8 131.5 %all-gather.20.cloned.1.call-start = ((), (), s32[]{:S(2)}) async-start(), calls=%async_computation.11 | async-start | bytes 2359296 | tf_op jit(solution)/shard_map/all_gather | solution.py:80
  439.6 131.8 %all-gather.22.cloned.1.call-start = ((), (), s32[]{:S(2)}) async-start(), calls=%async_computation.12 | async-start | bytes 2359296 | tf_op jit(solution)/shard_map/all_gather | solution.py:80
Sparse Core Ops, SparseCore 0:
  9.4 45.3 all-gather.11
  149.8 34.2 all-gather.13
  246.1 34.5 all-gather.15
  342.9 34.5 all-gather.17
  439.7 34.5 all-gather.19
  536.7 34.5 all-gather.21
where the time goes:
time: 675 us; the launch traced here: 664 us
  blocking collectives  253 us (37%)
  waiting for transfers between devices  210 us (31%)
  other arithmetic  127 us (19%)
  matrix products  37.3 us (6%)
  local copies, waits for them, and re-layouts  22.1 us (3%)
  between operations  14.2 us (2%)
    all_gather x5, waiting for transfers between devices, on_device(): column = lax.all_gather(panel_piece, 'row', axis=0, tiled=True)  169 us
    all_to_all x6, blocking collectives, sent_to_all(): lax.all_to_all(jnp.broadcast_to(shard[None], (length, *shard.shape)), axi...  142 us
    another operation x15, other arithmetic, on_device(): factor_block = jnp.linalg.cholesky(column[offset:offset + BLK])  61.9 us
    all_gather x5, blocking collectives, from_root(): lax.all_gather(shard, axis)  58.3 us
    all_to_all x1, blocking collectives, sum_at_owner(): lax.all_to_all(parts, axis, split_axis=0, concat_axis=0, tiled=True)  53.1 us
    another operation x10, other arithmetic, on_device(): lax.linalg.triangular_solve(factor_block, column, left_side=False, lower=...  52.3 us
    all_gather x1, waiting for transfers between devices, on_device(): every_block = lax.all_gather(transforms, 'row', axis=1, tiled=True)[0]  39.9 us
    another operation x5, matrix products, on_device(): lax.linalg.triangular_solve(factor_block, column, left_side=False, lower=...  26.2 us
  transfers between devices with their start and end apart: 6, of which 6 were waited for; matrix products, arithmetic and copies ran while one was open for 2% of the time, Pallas kernels for 0%

commit v1 on v0

v1 whole, which is shorter than its diff:
```python
import functools

import jax
import jax.numpy as jnp
from jax import lax
from jax.experimental import pallas as pl
from jax.experimental.pallas import tpu as pltpu
from jax.sharding import PartitionSpec as P

BLK = 128
NPAN = 5
STEP = 8
MESH = pl.DeviceIdType.MESH
HIGHEST = lax.Precision.HIGHEST
VMEM = pl.BlockSpec(memory_space=pltpu.VMEM)
PAIRS = [(i, j) for i in range(NPAN) for j in range(i, NPAN)]
NPAIR = len(PAIRS)


def f32(*shape):
    return jax.ShapeDtypeStruct(shape, jnp.float32)


def place():
    grp = lax.axis_index("grp")
    col = lax.axis_index("col")
    return dict(
        g=grp, y=grp // 2, xl=grp % 2, z=lax.axis_index("row"), c=col, xh=col // 2, core=col % 2
    )


def remote(src, dst, send, recv, **where):
    return pltpu.make_async_remote_copy(
        src_ref=src, dst_ref=dst, send_sem=send, recv_sem=recv, device_id=where, device_id_type=MESH
    )


def arrived(dst, send, recv):
    remote(dst, dst, send, recv, grp=lax.axis_index("grp")).wait_recv()


def meet(partners):
    barrier = pltpu.get_barrier_semaphore()
    for where in partners:
        pl.semaphore_signal(barrier, inc=1, device_id=where, device_id_type=MESH)
    pl.semaphore_wait(barrier, len(partners))


def params(ident):
    return pltpu.CompilerParams(collective_id=ident, has_side_effects=True, vmem_limit_bytes=40 << 20)


def spread_transforms_kernel(own, out, send_r, send_l, recv, sem):
    me = place()
    z, c, core = me["z"], me["c"], me["core"]
    right, left = (z + 1) % 8, (z + 7) % 8
    reach = 4 - core
    meet([{"row": right}, {"row": left}])
    for part in range(4):
        for slot in range(2):
            index = slot * 4 + part
            away = (z - (2 * c + slot) + 8) % 8
            here = out.at[index]

            def copy(src, sends, to):
                return remote(src, here, sends.at[index], recv.at[index], row=to)

            @pl.when(away == 0)
            def _():
                copy(own.at[part], send_r, right).start()
                copy(own.at[part], send_l, left).start()
                out[index] = own[part]

            @pl.when(away != 0)
            def _():
                arrived(here, send_r.at[index], recv.at[index])

            @pl.when((away > 0) & (away < reach))
            def _():
                copy(here, send_r, right).start()

            @pl.when(away > reach + 1)
            def _():
                copy(here, send_l, left).start()

    for part in range(4):
        for slot in range(2):
            index = slot * 4 + part
            away = (z - (2 * c + slot) + 8) % 8
            here = out.at[index]

            @pl.when(away < reach)
            def _():
                remote(here, here, send_r.at[index], recv.at[index], row=right).wait_send()

            @pl.when((away > reach + 1) | (away == 0))
            def _():
                remote(here, here, send_l.at[index], recv.at[index], row=left).wait_send()


def spread_transforms(own):
    return pl.pallas_call(
        spread_transforms_kernel,
        out_shape=f32(8, BLK, BLK),
        in_specs=[VMEM],
        out_specs=VMEM,
        scratch_shapes=[pltpu.SemaphoreType.DMA((8,))] * 3 + [pltpu.SemaphoreType.DMA],
        compiler_params=params(1),
    )(own)


def transform_kernel(rows, cols, normal, row_t, col_t, out, half):
    i = pl.program_id(0)
    left = row_t[rows[i]].T
    moved = jnp.dot(left, normal[...], precision=HIGHEST, preferred_element_type=jnp.float32)
    for b in range(8):
        half[b] = moved[:, b * BLK : (b + 1) * BLK]
    for j in range(8):
        b = cols[j]
        out[0, j] = jnp.dot(half[b], col_t[b], precision=HIGHEST, preferred_element_type=jnp.float32)


def transform(normal, row_t, col_t, rows, cols):
    return pl.pallas_call(
        transform_kernel,
        out_shape=f32(4, 8, BLK, BLK),
        grid_spec=pltpu.PrefetchScalarGridSpec(
            num_scalar_prefetch=2,
            grid=(4,),
            in_specs=[
                pl.BlockSpec((BLK, 1024), lambda i, r, c: (r[i], 0)),
                pl.BlockSpec((4, BLK, BLK), lambda i, r, c: (0, 0, 0)),
                pl.BlockSpec((8, BLK, BLK), lambda i, r, c: (0, 0, 0)),
            ],
            out_specs=pl.BlockSpec((1, 8, BLK, BLK), lambda i, r, c: (i, 0, 0, 0)),
            scratch_shapes=[pltpu.VMEM((8, BLK, BLK), jnp.float32)],
        ),
        compiler_params=pltpu.CompilerParams(vmem_limit_bytes=40 << 20),
    )(rows, cols, normal, row_t, col_t)


def leading_kernel(moved, out, parts, extra, total, s1, r1, se, re, s2, r2, s3, r3, s4, r4):
    me = place()
    g, z, c, xh, core = me["g"], me["z"], me["c"], me["xh"], me["core"]
    first = (z == 0) & (c == 0)
    partners = [{"grp": (g + d) % 16} for d in range(1, 16)]
    partners += [{"row": (z + d) % 8} for d in range(1, 8)]
    partners += [{"col": c ^ 1}, {"col": c ^ 2}]
    meet(partners)
    last = PAIRS.index((4, 4))

    @pl.when((z == 1) & (c == 0))
    def _():
        remote(moved.at[0, 4], extra, se, re, row=0).start()
        remote(moved.at[0, 4], extra, se, re, row=0).wait_send()

    @pl.when(first)
    def _():
        for t, (i, j) in enumerate(PAIRS):
            if t == last:
                arrived(extra, se, re)
                src = extra
            else:
                src = moved.at[i, j]

            @pl.when(g != t)
            def _():
                remote(src, parts.at[g], s1.at[t], r1.at[g], grp=t).start()

            @pl.when(g == t)
            def _():
                total[...] = src[...]

        @pl.when(g < NPAIR)
        def _():
            for d in range(1, 16):
                arrived(parts.at[(g + d) % 16], s1.at[0], r1.at[(g + d) % 16])
            acc = total[...]
            for d in range(1, 16):
                acc = acc + parts[(g + d) % 16]
            total[...] = acc
            out[g] = acc

        for t, (i, j) in enumerate(PAIRS):
            @pl.when(g != t)
            def _():
                remote(extra, parts.at[g], s1.at[t], r1.at[g], grp=t).wait_send()

    @pl.when(g < NPAIR)
    def _():
        @pl.when((z == 0) & (core == 0))
        def _():
            @pl.when(c == 0)
            def _():
                remote(total, out.at[g], s2.at[0], r2, col=2).start()
                for d in range(1, 8):
                    remote(total, out.at[g], s2.at[d], r2, row=(z + d) % 8).start()
                for d in range(8):
                    remote(total, out.at[g], s2.at[d], r2, row=(z + 1) % 8).wait_send()

            @pl.when(c == 2)
            def _():
                arrived(out.at[g], s2.at[0], r2)
                for d in range(1, 8):
                    remote(out.at[g], out.at[g], s2.at[d], r2, row=(z + d) % 8).start()
                for d in range(1, 8):
                    remote(out.at[g], out.at[g], s2.at[d], r2, row=(z + 1) % 8).wait_send()

        @pl.when((z != 0) & (core == 0))
        def _():
            arrived(out.at[g], s2.at[0], r2)

    @pl.when(core == 0)
    def _():
        @pl.when(g < NPAIR)
        def _():
            for d in (8, 7, 9, 6, 10, 5, 11, 4, 12, 3, 13, 2, 14, 1, 15):
                remote(out.at[g], out.at[g], s3.at[d], r3.at[g], grp=(g + d) % 16).start()
            remote(out.at[g], out.at[g], s4.at[0], r4.at[g], col=c ^ 1).start()
        for d in range(1, 16):
            t = (g + d) % 16

            @pl.when(t < NPAIR)
            def _():
                arrived(out.at[t], s3.at[0], r3.at[t])
                remote(out.at[t], out.at[t], s4.at[d], r4.at[t], col=c ^ 1).start()

        @pl.when(g < NPAIR)
        def _():
            for d in range(1, 16):
                remote(out.at[g], out.at[g], s3.at[d], r3.at[g], grp=(g + d) % 16).wait_send()
        for d in range(16):
            t = (g + d) % 16

            @pl.when(t < NPAIR)
            def _():
                remote(out.at[t], out.at[t], s4.at[d], r4.at[t], col=c ^ 1).wait_send()

    @pl.when(core == 1)
    def _():
        for t in range(NPAIR):
            arrived(out.at[t], s4.at[0], r4.at[t])


def leading(moved):
    dma = pltpu.SemaphoreType.DMA
    return pl.pallas_call(
        leading_kernel,
        out_shape=f32(NPAIR, BLK, BLK),
        in_specs=[VMEM],
        out_specs=VMEM,
        scratch_shapes=[
            pltpu.VMEM((16, BLK, BLK), jnp.float32),
            pltpu.VMEM((BLK, BLK), jnp.float32),
            pltpu.VMEM((BLK, BLK), jnp.float32),
            dma((16,)), dma((16,)), dma, dma, dma((8,)), dma, dma((16,)), dma((16,)), dma((16,)), dma((16,)),
        ],
        compiler_params=params(2),
    )(moved)


def add_up_kernel(moved, out, half, mine, parts, sx, rx, sy, ry):
    me = place()
    g, y, xl = me["g"], me["y"], me["xl"]
    order = (4, 1, 7, 2, 6, 3, 5, 0)
    meet([{"grp": g ^ 1}] + [{"grp": (g + 2 * d) % 16} for d in range(1, 8)])

    def across(d):
        b = (y + d) % 8
        return remote(moved.at[pl.ds(2 * (1 - xl), 2), b], half.at[b], sx.at[d], rx.at[d], grp=g ^ 1)

    def along(d):
        b = (y + d) % 8
        return remote(mine.at[b], parts.at[d], sy.at[d], ry.at[d], grp=(g + 2 * d) % 16)

    for d in order:
        across(d).start()
    for d in order:
        b = (y + d) % 8
        across(d).wait_recv()
        mine[b] = moved[pl.ds(2 * xl, 2), b] + half[b]
        if d:
            along(d).start()
    acc = mine[y]
    for d in order[:-1]:
        along(d).wait_recv()
        acc = acc + parts[d]
    out[...] = acc
    for d in order:
        across(d).wait_send()
        if d:
            along(d).wait_send()


def add_up(moved):
    dma = pltpu.SemaphoreType.DMA
    return pl.pallas_call(
        add_up_kernel,
        out_shape=f32(2, BLK, BLK),
        in_specs=[VMEM],
        out_specs=VMEM,
        scratch_shapes=[pltpu.VMEM((8, 2, BLK, BLK), jnp.float32)] * 3 + [dma((8,))] * 4,
        compiler_params=params(3),
    )(moved)


def panels_kernel(own, by_row, by_col, sx, rr, sy, sc, rc_d2d, sz, rz, sl, rl):
    me = place()
    g, y, xl, z, c, core = me["g"], me["y"], me["xl"], me["z"], me["c"], me["core"]
    partners = [{"grp": (g + 2 * d) % 16} for d in range(1, 8)] + [{"grp": g ^ 1}]
    partners += [{"row": (z + d) % 8} for d in range(1, 8)] + [{"col": c ^ 1}, {"col": c ^ 2}]
    meet(partners)

    for src_z, src_xl, start, count in ((0, 0, 0, 2), (0, 1, 2, 2), (1, 0, 4, 1)):
        n = src_z * 2 + src_xl
        there = by_col.at[pl.ds(start, count)]
        src = own.at[pl.ds(0, count)]

        @pl.when((z == src_z) & (xl == src_xl))
        def _():
            for d in range(1, 8):
                remote(src, there, sz.at[n, d], rz.at[n], row=(z + d) % 8).start()
            remote(src, there, sl.at[n], rl.at[n], grp=g ^ 1).start()
            by_col[start : start + count] = own[0:count]

    @pl.when((c == 0) & (y < NPAN))
    def _():
        remote(own, by_row.at[y], sx, rr.at[y], col=2).start()
        for d in (4, 3, 5, 2, 6, 1, 7):
            remote(own, by_row.at[y], sy.at[d], rr.at[y], grp=(g + 2 * d) % 16).start()
        by_row[y] = own[...]

    @pl.when((c == 2) & (y < NPAN))
    def _():
        arrived(by_row.at[y], sx, rr.at[y])
        for d in (4, 3, 5, 2, 6, 1, 7):
            remote(by_row.at[y], by_row.at[y], sy.at[d], rr.at[y], grp=(g + 2 * d) % 16).start()

    @pl.when(core == 0)
    def _():
        for k in range(NPAN):
            @pl.when((y == k) & (c == 0))
            def _():
                remote(own, by_row.at[k], sc.at[k], rc_d2d.at[k], col=c ^ 1).start()

            @pl.when((y == k) & (c == 2))
            def _():
                remote(by_row.at[k], by_row.at[k], sc.at[k], rc_d2d.at[k], col=c ^ 1).start()

            @pl.when(y != k)
            def _():
                arrived(by_row.at[k], sx, rr.at[k])
                remote(by_row.at[k], by_row.at[k], sc.at[k], rc_d2d.at[k], col=c ^ 1).start()

    for src_z, src_xl, start, count in ((0, 0, 0, 2), (0, 1, 2, 2), (1, 0, 4, 1)):
        n = src_z * 2 + src_xl
        there = by_col.at[pl.ds(start, count)]

        @pl.when((z != src_z) & (xl == src_xl))
        def _():
            arrived(there, sz.at[n, 0], rz.at[n])
            remote(there, there, sl.at[n], rl.at[n], grp=g ^ 1).start()

        @pl.when(xl != src_xl)
        def _():
            arrived(there, sl.at[n], rl.at[n])

    @pl.when(core == 1)
    def _():
        for k in range(NPAN):
            arrived(by_row.at[k], sc.at[k], rc_d2d.at[k])

    for src_z, src_xl, start, count in ((0, 0, 0, 2), (0, 1, 2, 2), (1, 0, 4, 1)):
        n = src_z * 2 + src_xl
        there = by_col.at[pl.ds(start, count)]

        @pl.when(xl == src_xl)
        def _():
            @pl.when(z == src_z)
            def _():
                for d in range(1, 8):
                    remote(there, there, sz.at[n, d], rz.at[n], row=(z + d) % 8).wait_send()
            remote(there, there, sl.at[n], rl.at[n], grp=g ^ 1).wait_send()

    @pl.when((core == 0) & (y < NPAN))
    def _():
        @pl.when(c == 0)
        def _():
            remote(own, by_row.at[y], sx, rr.at[y], col=2).wait_send()
        for d in range(1, 8):
            remote(own, by_row.at[y], sy.at[d], rr.at[y], grp=(g + 2 * d) % 16).wait_send()

    @pl.when(core == 0)
    def _():
        for k in range(NPAN):
            remote(own, by_row.at[k], sc.at[k], rc_d2d.at[k], col=c ^ 1).wait_send()


def panels(own):
    dma = pltpu.SemaphoreType.DMA
    return pl.pallas_call(
        panels_kernel,
        out_shape=(f32(NPAN, 2, BLK, BLK), f32(NPAN, BLK, BLK)),
        in_specs=[VMEM],
        out_specs=(VMEM, VMEM),
        scratch_shapes=[
            dma, dma((NPAN,)), dma((8,)), dma((NPAN,)), dma((NPAN,)), dma((3, 8)), dma((3,)), dma((3,)), dma((3,)),
        ],
        compiler_params=params(4),
    )(own)


def factor_inverse(a):
    row_ids = lax.broadcasted_iota(jnp.int32, (BLK, BLK), 0)
    col_ids = lax.broadcasted_iota(jnp.int32, (BLK, BLK), 1)
    inv = jnp.where(row_ids == col_ids, 1.0, 0.0).astype(jnp.float32)
    done = []
    for start in range(0, BLK, STEP):
        rest = BLK - start
        cols = [jnp.broadcast_to(a[:, start + j : start + j + 1], (rest, BLK)) for j in range(STEP)]
        top_a, top_i = a[:STEP], inv[:STEP]
        rows_a, rows_i = [], []
        for j in range(STEP):
            scale = lax.rsqrt(cols[j][j : j + 1])
            cols[j] = cols[j] * scale
            row_a, row_i = top_a[j : j + 1] * scale, top_i[j : j + 1] * scale
            rows_a.append(row_a)
            rows_i.append(row_i)
            if j + 1 < STEP:
                low = cols[j][:STEP]
                top_a = top_a - low * row_a
                top_i = top_i - low * row_i
                for k in range(j + 1, STEP):
                    cols[k] = cols[k] - cols[j][k : k + 1] * cols[j]
        done.append(jnp.concatenate(rows_i, axis=0))
        if rest > STEP:
            a, inv = a[STEP:], inv[STEP:]
            for j in range(STEP):
                low = cols[j][STEP:]
                a = a - low * rows_a[j]
                inv = inv - low * rows_i[j]
    return jnp.concatenate(done, axis=0)


def mm(a, b):
    return jnp.dot(a, b, precision=HIGHEST, preferred_element_type=jnp.float32)


def mm_nt(a, b):
    return lax.dot_general(
        a, b, (((1,), (1,)), ((), ())), precision=HIGHEST, preferred_element_type=jnp.float32
    )


def eliminate_kernel(lead, by_row, by_col, own, out, square, upper, rows, cols):
    me = place()
    row_block = 4 * me["z"] + 2 * me["xl"]
    col_block = 8 * me["c"] + me["y"]
    for t, (i, j) in enumerate(PAIRS):
        square[i, j] = lead[t]
    rows[...] = by_row[...]
    cols[...] = by_col[...]
    out[...] = own[...]

    def panel(k, carry):
        inverse = factor_inverse(square[k, k])
        col_factor = mm(inverse, cols[k])
        row_factor = mm_nt(rows[k].reshape(2 * BLK, BLK), inverse)
        which = row_block + lax.broadcasted_iota(jnp.int32, (2 * BLK, BLK), 0) // BLK
        row_factor = jnp.where(which >= k, row_factor, 0.0)

        def solve(j, carry):
            upper[j] = mm(inverse, square[k, j])
            return carry

        lax.fori_loop(k + 1, NPAN, solve, 0)

        def update(i, carry):
            flipped = upper[i].T

            def inner(j, carry):
                square[i, j] -= mm(flipped, upper[j])
                return carry

            lax.fori_loop(i, NPAN, inner, 0)
            cols[i] -= mm(flipped, col_factor)
            rows[i] -= mm(row_factor, upper[i]).reshape(2, BLK, BLK)
            return carry

        lax.fori_loop(k + 1, NPAN, update, 0)

        @pl.when(col_block >= NPAN)
        def _():
            out[...] -= mm(row_factor, col_factor).reshape(2, BLK, BLK)

        @pl.when(col_block == k)
        def _():
            out[...] = row_factor.reshape(2, BLK, BLK)

        return carry

    lax.fori_loop(0, NPAN, panel, 0)


def eliminate(lead, by_row, by_col, own):
    return pl.pallas_call(
        eliminate_kernel,
        out_shape=f32(2, BLK, BLK),
        in_specs=[VMEM] * 4,
        out_specs=VMEM,
        scratch_shapes=[
            pltpu.VMEM((NPAN, NPAN, BLK, BLK), jnp.float32),
            pltpu.VMEM((NPAN, BLK, BLK), jnp.float32),
            pltpu.VMEM((NPAN, 2, BLK, BLK), jnp.float32),
            pltpu.VMEM((NPAN, BLK, BLK), jnp.float32),
        ],
        compiler_params=pltpu.CompilerParams(vmem_limit_bytes=40 << 20),
    )(lead, by_row, by_col, own)


def collect_kernel(own, out, sy, ry, sx, rx):
    me = place()
    g, y, xl = me["g"], me["y"], me["xl"]
    order = (1, 7, 2, 6, 3, 5, 4)
    meet([{"grp": g ^ 1}] + [{"grp": (g + 2 * d) % 16} for d in range(1, 8)])

    def spot(x, d):
        col = pl.multiple_of(((y - d + 8) % 8) * BLK, BLK)
        return out.at[pl.ds(pl.multiple_of(x * 2 * BLK, BLK), 2 * BLK), pl.ds(col, BLK)]

    def along(d):
        return remote(own, spot(xl, 0), sy.at[d], ry.at[d], grp=(g + 2 * d) % 16)

    def across(d, src):
        return remote(src, spot(xl, d), sx.at[d], rx.at[d], grp=g ^ 1)

    for d in (4, 3, 5, 2, 6, 1, 7):
        along(d).start()
    across(0, own).start()
    mine = pl.ds(pl.multiple_of(xl * 2 * BLK, BLK), 2 * BLK)
    out[mine, pl.ds(pl.multiple_of(y * BLK, BLK), BLK)] = own[...]
    for d in order:
        arrived(spot(xl, d), sy.at[d], ry.at[d])
        across(d, spot(xl, d)).start()
    for d in (0,) + order:
        arrived(spot(1 - xl, d), sx.at[d], rx.at[d])
    for d in (0,) + order:
        across(d, own).wait_send()
        if d:
            along(d).wait_send()


def collect(own):
    dma = pltpu.SemaphoreType.DMA
    return pl.pallas_call(
        collect_kernel,
        out_shape=f32(4 * BLK, 8 * BLK),
        in_specs=[VMEM],
        out_specs=VMEM,
        scratch_shapes=[dma((8,))] * 4,
        compiler_params=params(5),
    )(own)


def on_device(normals, transforms, block_map):
    row = lax.axis_index("row")
    col = lax.axis_index("col")
    mapping = block_map[0]
    row_map = lax.dynamic_slice_in_dim(mapping, row * 4, 4, 0) - row * 4
    col_map = lax.dynamic_slice_in_dim(mapping, col * 8, 8, 0) - col * 8
    col_transforms = spread_transforms(transforms[0])
    moved = transform(normals[0], transforms[0], col_transforms, row_map, col_map)
    lead = leading(moved)
    own = add_up(moved)
    by_row, by_col = panels(own)
    done = eliminate(lead, by_row, by_col, own)
    return collect(done.reshape(2 * BLK, BLK))


def solution(mesh):
    return jax.shard_map(
        on_device,
        mesh=mesh,
        in_specs=(P("grp", "row", "col"), P("grp", "row", None, None), P("grp", None)),
        out_specs=P("row", "col"),
        check_vma=False,
    )
```

time: 675 us -> 239 us (0.35)
  the two profiles are of different devices: /device:TPU:1 before, /device:TPU:4 now
where the time goes in v1:
time: 239 us
  Pallas kernels  233 us (97%)
  local copies, waits for them, and re-layouts  3.86 us (2%)
    pallas_call x1, Pallas kernels, collect(): pl.pallas_call(collect_kernel, out_shape=f32(4 * BLK, 8 * BLK), in_specs=...  51.6 us
    pallas_call x1, Pallas kernels, leading(): pl.pallas_call(leading_kernel, out_shape=f32(NPAIR, BLK, BLK), in_specs=[...  47.2 us
    pallas_call x1, Pallas kernels, spread_transforms(): pl.pallas_call(spread_transforms_kernel, out_shape=f32(8, BLK, BLK), in_s...  44.7 us
    pallas_call x1, Pallas kernels, eliminate(): pl.pallas_call(eliminate_kernel, out_shape=f32(2, BLK, BLK), in_specs=[VM...  33.6 us
    pallas_call x1, Pallas kernels, panels(): pl.pallas_call(panels_kernel, out_shape=(f32(NPAN, 2, BLK, BLK), f32(NPAN...  25.9 us
    pallas_call x1, Pallas kernels, add_up(): pl.pallas_call(add_up_kernel, out_shape=f32(2, BLK, BLK), in_specs=[VMEM]...  24.8 us
    pallas_call x1, Pallas kernels, transform(): pl.pallas_call(transform_kernel, out_shape=f32(4, 8, BLK, BLK), grid_spec...  5.43 us

profile of v1, /device:TPU:4, one launch (start us, length us, event | category | flops | bytes accessed | tf_op | source)
XLA Modules:
  0.0 238.6 jit_solution(9463351394018822494)
XLA Ops:
  0.0 0.7 subtract_bitcast_fusion.cols
  0.7 0.7 subtract_bitcast_fusion.1.rows
  1.5 0.0 copy-start.1
  1.5 0.9 copy-done.1
  2.4 44.7 %shard_map.37.col_t = f32[8,128,128]{2,1,0:T(8,128)S(1)} custom-call(f32[4,128,128]{2,1,0:T(8,128)S(1)} %bitcast.8), custom_call_target="tpu_custom_call" | custom-call | tf_op jit(solution)/shard_map/pallas_call | solution.py:102
  47.1 0.0 copy-start
  47.1 1.6 copy-done
  48.7 5.4 %shard_map.38.moved = f32[4,8,128,128]{3,2,1,0:T(8,128)S(1)} custom-call(s32[4]{0:T(128)S(1)} %subtract_bitcast_fusion.1.rows, s32[8]{0:T(128)S(1)} %subtract_bitcast_fusion.cols, f32[512,1024]{1,0:T(8,128)S(1)} %bitcast.7, f32[4,128,128]{2,1,0:T(8,128)S(1)} %bitcast.9, f32[8,128,128]{2,1,0:T(8,128)S(1)} %shard_map.37.col_t), custom_call_target="tpu_custom_call" | custom-call | tf_op jit(solution)/shard_map/pallas_call | solution.py:124
  54.1 24.8 %shard_map.40.own = f32[2,128,128]{2,1,0:T(8,128)S(1)} custom-call(f32[4,8,128,128]{3,2,1,0:T(8,128)S(1)} %shard_map.38.moved), custom_call_target="tpu_custom_call" | custom-call | tf_op jit(solution)/shard_map/pallas_call | solution.py:297
  78.9 47.2 %shard_map.39.lead = f32[15,128,128]{2,1,0:T(8,128)S(1)} custom-call(f32[4,8,128,128]{3,2,1,0:T(8,128)S(1)} %shard_map.38.moved), custom_call_target="tpu_custom_call" | custom-call | tf_op jit(solution)/shard_map/pallas_call | solution.py:247
  126.1 25.9 %shard_map.41 = (f32[5,2,128,128]{3,2,1,0:T(8,128)S(1)}, f32[5,128,128]{2,1,0:T(8,128)S(1)}) custom-call(f32[2,128,128]{2,1,0:T(8,128)S(1)} %shard_map.40.own), custom_call_target="tpu_custom_call" | custom-call | tf_op jit(solution)/shard_map/pallas_call | solution.py:401
  152.1 33.6 %shard_map.42 = f32[2,128,128]{2,1,0:T(8,128)S(1)} custom-call(f32[15,128,128]{2,1,0:T(8,128)S(1)} %shard_map.39.lead, f32[5,2,128,128]{3,2,1,0:T(8,128)S(1)} %get-tuple-element.7.by_row, f32[5,128,128]{2,1,0:T(8,128)S(1)} %get-tuple-element.8.by_col, f32[2,128,128]{2,1,0:T(8,128)S(1)} %shard_map.40.own), custom_call_target="tpu_custom_call" | custom-call | tf_op jit(solution)/shard_map/pallas_call | solution.py:506
  185.6 51.6 %shard_map.43 = f32[512,1024]{1,0:T(8,128)S(1)} custom-call(f32[256,128]{1,0:T(8,128)S(1)} %bitcast.10), custom_call_target="tpu_custom_call" | custom-call | tf_op jit(solution)/shard_map/pallas_call | solution.py:555
  237.3 1.3 copy.5
Async XLA Ops:
  1.5 0.9 copy-start.1
  47.1 1.6 copy-start

commit v2 on v1

v2 whole, which is shorter than its diff:
```python
import functools

import jax
import jax.numpy as jnp
from jax import lax
from jax.experimental import pallas as pl
from jax.experimental.pallas import tpu as pltpu
from jax.sharding import PartitionSpec as P

BLK = 128
NPAN = 5
STEP = 8
MESH = pl.DeviceIdType.MESH
HIGHEST = lax.Precision.HIGHEST
VMEM = pl.BlockSpec(memory_space=pltpu.VMEM)
PAIRS = [(i, j) for i in range(NPAN) for j in range(i, NPAN)]
NPAIR = len(PAIRS)


def f32(*shape):
    return jax.ShapeDtypeStruct(shape, jnp.float32)


def place():
    grp = lax.axis_index("grp")
    col = lax.axis_index("col")
    return dict(
        g=grp, y=grp // 2, xl=grp % 2, z=lax.axis_index("row"), c=col, xh=col // 2, core=col % 2
    )


def remote(src, dst, send, recv, **where):
    return pltpu.make_async_remote_copy(
        src_ref=src, dst_ref=dst, send_sem=send, recv_sem=recv, device_id=where, device_id_type=MESH
    )


def arrived(dst, send, recv):
    remote(dst, dst, send, recv, grp=lax.axis_index("grp")).wait_recv()


def meet(partners):
    barrier = pltpu.get_barrier_semaphore()
    for where in partners:
        pl.semaphore_signal(barrier, inc=1, device_id=where, device_id_type=MESH)
    pl.semaphore_wait(barrier, len(partners))


def params(ident):
    return pltpu.CompilerParams(collective_id=ident, has_side_effects=True, vmem_limit_bytes=40 << 20)


FAR = (4, 3, 5, 2, 6, 1, 7)
GRP_FAR = (8, 7, 9, 6, 10, 5, 11, 4, 12, 3, 13, 2, 14, 1, 15)
COL_SOURCES = ((0, 0, 0, 2), (0, 1, 2, 2), (1, 0, 4, 1))


def dot(a, b):
    return jnp.dot(a, b, precision=HIGHEST, preferred_element_type=jnp.float32)


def gather_kernel(
    mapping, own_t, normal_hbm, lead, own, by_row, by_col,
    normal, col_t, left, moved, half, mine, parts, lparts, extra, total,
    sem, send_r, send_l, recv, sx, rx, sy, ry,
    s1, r1, se, re, s2, r2, s3, r3, s4, r4, spx, rr, spy, sc, rcd, sz, rz, sl, rl,
):
    me = place()
    g, y, xl, z, c, core = me["g"], me["y"], me["xl"], me["z"], me["c"], me["core"]
    fetch = pltpu.make_async_copy(normal_hbm, normal, sem)
    fetch.start()
    meet(
        [{"grp": (g + d) % 16} for d in range(1, 16)]
        + [{"row": (z + d) % 8} for d in range(1, 8)]
        + [{"col": c ^ 1}, {"col": c ^ 2}]
    )

    up, down = (z + 1) % 8, (z + 7) % 8
    reach = 4 - core

    def away_of(slot):
        return (z - (2 * c + slot) + 8) % 8

    def spread(index, src, sends, to):
        return remote(src, col_t.at[index], sends.at[index], recv.at[index], row=to)

    for slot in range(2):
        @pl.when(away_of(slot) == 0)
        def _():
            for part in range(4):
                index = slot * 4 + part
                spread(index, own_t.at[part], send_r, up).start()
                spread(index, own_t.at[part], send_l, down).start()
                col_t[index] = own_t[part]

    fetch.wait()
    for i in range(4):
        block = mapping[0, 4 * z + i] % 4
        turned = dot(own_t[block].T, normal[block])
        for b in range(8):
            left[b, i * BLK : (i + 1) * BLK, :] = turned[:, b * BLK : (b + 1) * BLK]

    rising = (away_of(1) <= reach).astype(jnp.int32)
    for part in range(4):
        for turn in range(2):
            slot = (rising + turn) % 2
            index = slot * 4 + part
            away = away_of(slot)

            @pl.when(away != 0)
            def _():
                arrived(col_t.at[index], send_r.at[index], recv.at[index])

            @pl.when((away > 0) & (away < reach))
            def _():
                spread(index, col_t.at[index], send_r, up).start()

            @pl.when(away > reach + 1)
            def _():
                spread(index, col_t.at[index], send_l, down).start()

    order = (4, 1, 7, 2, 6, 3, 5, 0)

    def across(d):
        b = (y + d) % 8
        return remote(
            moved.at[b, pl.ds(2 * (1 - xl), 2)], half.at[b], sx.at[d], rx.at[d], grp=g ^ 1
        )

    def along(d):
        b = (y + d) % 8
        return remote(mine.at[b], parts.at[d], sy.at[d], ry.at[d], grp=(g + 2 * d) % 16)

    for d in order:
        j = (y + d) % 8
        b = j // 4 * 4 + mapping[0, 8 * c + j] % 4
        moved[j] = dot(left[b], col_t[b]).reshape(4, BLK, BLK)
        across(d).start()

    first = (z == 0) & (c == 0)
    last = PAIRS.index((4, 4))

    @pl.when((z == 1) & (c == 0))
    def _():
        remote(moved.at[4, 0], extra, se, re, row=0).start()

    @pl.when(first)
    def _():
        for t, (i, j) in enumerate(PAIRS):
            if t == last:
                arrived(extra, se, re)
                src = extra
            else:
                src = moved.at[j, i]

            @pl.when(g != t)
            def _():
                remote(src, lparts.at[g], s1.at[t], r1.at[g], grp=t).start()

            @pl.when(g == t)
            def _():
                total[...] = src[...]

    for d in order:
        b = (y + d) % 8
        across(d).wait_recv()
        mine[b] = moved[b, pl.ds(2 * xl, 2)] + half[b]
        if d:
            along(d).start()

    @pl.when(first & (g < NPAIR))
    def _():
        for d in range(1, 16):
            arrived(lparts.at[(g + d) % 16], s1.at[0], r1.at[(g + d) % 16])
        acc = total[...]
        for d in range(1, 16):
            acc = acc + lparts[(g + d) % 16]
        total[...] = acc
        lead[g] = acc
        remote(total, lead.at[g], s2.at[0], r2, col=2).start()
        for d in FAR:
            remote(total, lead.at[g], s2.at[d], r2, row=(z + d) % 8).start()

    @pl.when((z == 0) & (c == 2) & (g < NPAIR))
    def _():
        arrived(lead.at[g], s2.at[0], r2)
        for d in FAR:
            remote(lead.at[g], lead.at[g], s2.at[d], r2, row=(z + d) % 8).start()

    acc = mine[y]
    for d in order[:-1]:
        along(d).wait_recv()
        acc = acc + parts[d]
    own[...] = acc

    for src_z, src_xl, start, count in COL_SOURCES:
        n = src_z * 2 + src_xl
        there = by_col.at[pl.ds(start, count)]
        src = own.at[pl.ds(0, count)]

        @pl.when((z == src_z) & (xl == src_xl))
        def _():
            for d in FAR:
                remote(src, there, sz.at[n, d], rz.at[n], row=(z + d) % 8).start()
            remote(src, there, sl.at[n], rl.at[n], grp=g ^ 1).start()
            by_col[start : start + count] = own[0:count]

    @pl.when((c == 0) & (y < NPAN))
    def _():
        remote(own, by_row.at[y], spx, rr.at[y], col=2).start()
        for d in FAR:
            remote(own, by_row.at[y], spy.at[d], rr.at[y], grp=(g + 2 * d) % 16).start()
        remote(own, by_row.at[y], sc.at[y], rcd.at[y], col=c ^ 1).start()
        by_row[y] = own[...]

    @pl.when((core == 0) & (g < NPAIR))
    def _():
        @pl.when(z != 0)
        def _():
            arrived(lead.at[g], s2.at[0], r2)
        for d in GRP_FAR:
            remote(lead.at[g], lead.at[g], s3.at[d], r3.at[g], grp=(g + d) % 16).start()
        remote(lead.at[g], lead.at[g], s4.at[0], r4.at[g], col=c ^ 1).start()

    @pl.when((c == 2) & (y < NPAN))
    def _():
        arrived(by_row.at[y], spx, rr.at[y])
        for d in FAR:
            remote(by_row.at[y], by_row.at[y], spy.at[d], rr.at[y], grp=(g + 2 * d) % 16).start()
        remote(by_row.at[y], by_row.at[y], sc.at[y], rcd.at[y], col=c ^ 1).start()

    for src_z, src_xl, start, count in COL_SOURCES:
        n = src_z * 2 + src_xl
        there = by_col.at[pl.ds(start, count)]

        @pl.when((z != src_z) & (xl == src_xl))
        def _():
            arrived(there, sz.at[n, 0], rz.at[n])
            remote(there, there, sl.at[n], rl.at[n], grp=g ^ 1).start()

    @pl.when(core == 0)
    def _():
        for k in range(NPAN):
            @pl.when(y != k)
            def _():
                arrived(by_row.at[k], spx, rr.at[k])
                remote(by_row.at[k], by_row.at[k], sc.at[k], rcd.at[k], col=c ^ 1).start()
        for d in range(1, 16):
            t = (g + d) % 16

            @pl.when(t < NPAIR)
            def _():
                arrived(lead.at[t], s3.at[0], r3.at[t])
                remote(lead.at[t], lead.at[t], s4.at[d], r4.at[t], col=c ^ 1).start()

    for src_z, src_xl, start, count in COL_SOURCES:
        n = src_z * 2 + src_xl

        @pl.when(xl != src_xl)
        def _():
            arrived(by_col.at[pl.ds(start, count)], sl.at[n], rl.at[n])

    @pl.when(core == 1)
    def _():
        for k in range(NPAN):
            arrived(by_row.at[k], sc.at[k], rcd.at[k])
        for t in range(NPAIR):
            arrived(lead.at[t], s4.at[0], r4.at[t])

    for slot in range(2):
        away = away_of(slot)
        for part in range(4):
            index = slot * 4 + part

            @pl.when(away < reach)
            def _():
                spread(index, col_t.at[index], send_r, up).wait_send()

            @pl.when((away > reach + 1) | (away == 0))
            def _():
                spread(index, col_t.at[index], send_l, down).wait_send()
    for d in order:
        across(d).wait_send()
        if d:
            along(d).wait_send()

    @pl.when((z == 1) & (c == 0))
    def _():
        remote(extra, extra, se, re, row=0).wait_send()

    @pl.when(first)
    def _():
        for t in range(NPAIR):
            @pl.when(g != t)
            def _():
                remote(extra, lparts.at[g], s1.at[t], r1.at[g], grp=t).wait_send()

        @pl.when(g < NPAIR)
        def _():
            remote(total, lead.at[g], s2.at[0], r2, col=2).wait_send()

    @pl.when((z == 0) & (core == 0) & (g < NPAIR))
    def _():
        for d in FAR:
            remote(total, lead.at[g], s2.at[d], r2, row=(z + d) % 8).wait_send()

    for src_z, src_xl, start, count in COL_SOURCES:
        n = src_z * 2 + src_xl
        there = by_col.at[pl.ds(start, count)]

        @pl.when(xl == src_xl)
        def _():
            @pl.when(z == src_z)
            def _():
                for d in FAR:
                    remote(there, there, sz.at[n, d], rz.at[n], row=(z + d) % 8).wait_send()
            remote(there, there, sl.at[n], rl.at[n], grp=g ^ 1).wait_send()

    @pl.when(core == 0)
    def _():
        @pl.when(y < NPAN)
        def _():
            @pl.when(c == 0)
            def _():
                remote(own, by_row.at[y], spx, rr.at[y], col=2).wait_send()
            for d in FAR:
                remote(own, by_row.at[y], spy.at[d], rr.at[y], grp=(g + 2 * d) % 16).wait_send()
        for k in range(NPAN):
            remote(own, by_row.at[k], sc.at[k], rcd.at[k], col=c ^ 1).wait_send()

        @pl.when(g < NPAIR)
        def _():
            for d in GRP_FAR:
                remote(total, lead.at[g], s3.at[d], r3.at[g], grp=(g + d) % 16).wait_send()
        for d in range(16):
            t = (g + d) % 16

            @pl.when(t < NPAIR)
            def _():
                remote(total, lead.at[t], s4.at[d], r4.at[t], col=c ^ 1).wait_send()


def gather(mapping, own_t, normal):
    dma = pltpu.SemaphoreType.DMA

    def buf(*shape):
        return pltpu.VMEM(shape, jnp.float32)

    return pl.pallas_call(
        gather_kernel,
        out_shape=(f32(NPAIR, BLK, BLK), f32(2, BLK, BLK), f32(NPAN, 2, BLK, BLK), f32(NPAN, BLK, BLK)),
        in_specs=[pl.BlockSpec(memory_space=pltpu.SMEM), VMEM, pl.BlockSpec(memory_space=pl.ANY)],
        out_specs=(VMEM,) * 4,
        scratch_shapes=[
            buf(4, BLK, 8 * BLK), buf(8, BLK, BLK), buf(8, 4 * BLK, BLK), buf(8, 4, BLK, BLK),
            buf(8, 2, BLK, BLK), buf(8, 2, BLK, BLK), buf(8, 2, BLK, BLK),
            buf(16, BLK, BLK), buf(BLK, BLK), buf(BLK, BLK),
            dma, dma((8,)), dma((8,)), dma((8,)), dma((8,)), dma((8,)), dma((8,)), dma((8,)),
            dma((16,)), dma((16,)), dma, dma, dma((8,)), dma, dma((16,)), dma((16,)), dma((16,)), dma((16,)),
            dma, dma((NPAN,)), dma((8,)), dma((NPAN,)), dma((NPAN,)), dma((3, 8)), dma((3,)), dma((3,)), dma((3,)),
        ],
        compiler_params=params(1),
    )(mapping, own_t, normal)


def factor_inverse(a):
    row_ids = lax.broadcasted_iota(jnp.int32, (BLK, BLK), 0)
    col_ids = lax.broadcasted_iota(jnp.int32, (BLK, BLK), 1)
    inv = jnp.where(row_ids == col_ids, 1.0, 0.0).astype(jnp.float32)
    done = []
    for start in range(0, BLK, STEP):
        rest = BLK - start
        cols = [jnp.broadcast_to(a[:, start + j : start + j + 1], (rest, BLK)) for j in range(STEP)]
        top_a, top_i = a[:STEP], inv[:STEP]
        rows_a, rows_i = [], []
        for j in range(STEP):
            scale = lax.rsqrt(cols[j][j : j + 1])
            cols[j] = cols[j] * scale
            row_a, row_i = top_a[j : j + 1] * scale, top_i[j : j + 1] * scale
            rows_a.append(row_a)
            rows_i.append(row_i)
            if j + 1 < STEP:
                low = cols[j][:STEP]
                top_a = top_a - low * row_a
                top_i = top_i - low * row_i
                for k in range(j + 1, STEP):
                    cols[k] = cols[k] - cols[j][k : k + 1] * cols[j]
        done.append(jnp.concatenate(rows_i, axis=0))
        if rest > STEP:
            a, inv = a[STEP:], inv[STEP:]
            for j in range(STEP):
                low = cols[j][STEP:]
                a = a - low * rows_a[j]
                inv = inv - low * rows_i[j]
    return jnp.concatenate(done, axis=0)


def mm(a, b):
    return jnp.dot(a, b, precision=HIGHEST, preferred_element_type=jnp.float32)


def mm_nt(a, b):
    return lax.dot_general(
        a, b, (((1,), (1,)), ((), ())), precision=HIGHEST, preferred_element_type=jnp.float32
    )


def eliminate_kernel(lead, by_row, by_col, own, out, square, upper, rows, cols):
    me = place()
    row_block = 4 * me["z"] + 2 * me["xl"]
    col_block = 8 * me["c"] + me["y"]
    for t, (i, j) in enumerate(PAIRS):
        square[i, j] = lead[t]
    rows[...] = by_row[...]
    cols[...] = by_col[...]
    out[...] = own[...]

    def panel(k, carry):
        inverse = factor_inverse(square[k, k])
        col_factor = mm(inverse, cols[k])
        row_factor = mm_nt(rows[k].reshape(2 * BLK, BLK), inverse)
        which = row_block + lax.broadcasted_iota(jnp.int32, (2 * BLK, BLK), 0) // BLK
        row_factor = jnp.where(which >= k, row_factor, 0.0)

        def solve(j, carry):
            upper[j] = mm(inverse, square[k, j])
            return carry

        lax.fori_loop(k + 1, NPAN, solve, 0)

        def update(i, carry):
            flipped = upper[i].T

            def inner(j, carry):
                square[i, j] -= mm(flipped, upper[j])
                return carry

            lax.fori_loop(i, NPAN, inner, 0)
            cols[i] -= mm(flipped, col_factor)
            rows[i] -= mm(row_factor, upper[i]).reshape(2, BLK, BLK)
            return carry

        lax.fori_loop(k + 1, NPAN, update, 0)

        @pl.when(col_block >= NPAN)
        def _():
            out[...] -= mm(row_factor, col_factor).reshape(2, BLK, BLK)

        @pl.when(col_block == k)
        def _():
            out[...] = row_factor.reshape(2, BLK, BLK)

        return carry

    lax.fori_loop(0, NPAN, panel, 0)


def eliminate(lead, by_row, by_col, own):
    return pl.pallas_call(
        eliminate_kernel,
        out_shape=f32(2, BLK, BLK),
        in_specs=[VMEM] * 4,
        out_specs=VMEM,
        scratch_shapes=[
            pltpu.VMEM((NPAN, NPAN, BLK, BLK), jnp.float32),
            pltpu.VMEM((NPAN, BLK, BLK), jnp.float32),
            pltpu.VMEM((NPAN, 2, BLK, BLK), jnp.float32),
            pltpu.VMEM((NPAN, BLK, BLK), jnp.float32),
        ],
        compiler_params=pltpu.CompilerParams(vmem_limit_bytes=40 << 20),
    )(lead, by_row, by_col, own)


HOPS = {
    "R1": (0, 1), "R2": (0, 2), "R3": (0, 3), "R4": (0, 4), "L1": (0, -1), "L2": (0, -2), "L3": (0, -3),
    "P0": (1, 0), "RP1": (1, 1), "LP1": (1, -1), "LP2": (1, -2),
    "X2": (1, 2), "X3": (1, 3), "X4": (1, 4), "XL": (1, -3),
}
NAMES = list(HOPS)
ONWARD = {
    "own": (("P0", "x"), ("R1", "r"), ("L1", "l")),
    "P0": (("RP1", "r"), ("LP1", "l")),
    "R1": (("R2", "r"),),
    "L1": (("L2", "l"),),
    "R2": (("R3", "r"), ("X2", "x")),
    "L2": (("L3", "l"),),
    "LP1": (("LP2", "l"),),
    "R3": (("R4", "r"), ("X3", "x")),
    "L3": (("XL", "x"),),
    "R4": (("X4", "x"),),
    "RP1": (), "LP2": (), "X2": (), "XL": (), "X3": (), "X4": (),
}


def collect_kernel(own, out, send, recv):
    me = place()
    g, y, xl = me["g"], me["y"], me["xl"]
    to = {"x": g ^ 1, "r": (g + 2) % 16, "l": (g + 14) % 16}
    meet([{"grp": to["x"]}, {"grp": to["r"]}, {"grp": to["l"]}])

    def spot(x, steps, part):
        row = pl.multiple_of((x * 2 + part) * BLK, BLK)
        col = pl.multiple_of(((y - steps + 8) % 8) * BLK, BLK)
        return out.at[pl.ds(row, BLK), pl.ds(col, BLK)]

    def here(name, part):
        other, steps = HOPS[name]
        return spot(1 - xl if other else xl, steps, part)

    def hop(src_name, name, way, part):
        if src_name == "own":
            src, dst = own.at[part], spot(xl, 0, part)
        else:
            src = dst = here(src_name, part)
        n = NAMES.index(name)
        return remote(src, dst, send.at[n, part], recv.at[n, part], grp=to[way])

    for part in range(2):
        for name, way in ONWARD["own"]:
            hop("own", name, way, part).start()
        row = pl.multiple_of((xl * 2 + part) * BLK, BLK)
        out[pl.ds(row, BLK), pl.ds(pl.multiple_of(y * BLK, BLK), BLK)] = own[part]
    for src_name in list(ONWARD)[1:]:
        for part in range(2):
            n = NAMES.index(src_name)
            arrived(here(src_name, part), send.at[n, part], recv.at[n, part])
            for name, way in ONWARD[src_name]:
                hop(src_name, name, way, part).start()
    for src_name in ONWARD:
        for name, way in ONWARD[src_name]:
            for part in range(2):
                hop(src_name, name, way, part).wait_send()


def collect(own):
    dma = pltpu.SemaphoreType.DMA
    return pl.pallas_call(
        collect_kernel,
        out_shape=f32(4 * BLK, 8 * BLK),
        in_specs=[VMEM],
        out_specs=VMEM,
        scratch_shapes=[dma((15, 2))] * 2,
        compiler_params=params(2),
    )(own)


def on_device(normals, transforms, block_map):
    lead, own, by_row, by_col = gather(block_map, transforms[0], normals.reshape(4, BLK, 8 * BLK))
    return collect(eliminate(lead, by_row, by_col, own))


def solution(mesh):
    return jax.shard_map(
        on_device,
        mesh=mesh,
        in_specs=(P("grp", "row", "col"), P("grp", "row", None, None), P("grp", None)),
        out_specs=P("row", "col"),
        check_vma=False,
    )
```

time: 239 us -> 155 us (0.65)
  the two profiles are of different devices: /device:TPU:4 before, /device:TPU:1 now
where the time goes in v2:
time: 155 us; the launch traced here: 153 us
  Pallas kernels  149 us (96%)
  local copies, waits for them, and re-layouts  4.52 us (3%)
    pallas_call x1, Pallas kernels, gather(): pl.pallas_call(gather_kernel, out_shape=(f32(NPAIR, BLK, BLK), f32(2, BLK...  90.6 us
    pallas_call x1, Pallas kernels, eliminate(): pl.pallas_call(eliminate_kernel, out_shape=f32(2, BLK, BLK), in_specs=[VM...  33.6 us
    pallas_call x1, Pallas kernels, collect(): pl.pallas_call(collect_kernel, out_shape=f32(4 * BLK, 8 * BLK), in_specs=...  24.7 us
    unnamed x7, local copies, waits for them, and re-layouts  4.52 us

profile of v2, /device:TPU:1, one launch (start us, length us, event | category | flops | bytes accessed | tf_op | source)
XLA Modules:
  0.0 153.4 jit_solution(3085472060933905277)
XLA Ops:
  0.0 0.0 copy-start
  0.0 1.6 %copy-done = f32[1,512,1024]{2,1,0:T(8,128)S(1)} copy-done((f32[1,512,1024]{2,1,0:T(8,128)S(1)}, f32[1,512,1024]{2,1,0:T(8,128)}, u32[]{:S(2)}) %copy-start) | copy-done | bytes 2097176
  1.6 0.0 copy-start.1
  1.6 0.9 copy-done.1
  2.5 0.0 copy-start.2
  2.5 0.7 copy-done.2
  3.2 90.6 %shard_map.37 = (f32[15,128,128]{2,1,0:T(8,128)S(1)}, f32[2,128,128]{2,1,0:T(8,128)S(1)}, f32[5,2,128,128]{3,2,1,0:T(8,128)S(1)}, f32[5,128,128]{2,1,0:T(8,128)S(1)}) custom-call(s32[1,32]{1,0:T(1,128)S(1)} %copy-done.2, f32[4,128,128]{2,1,0:T(8,128)S(1)} %bitcast.3, f32[4,128,1024]{2,1,0:T(8,128)S(1)} %bitcast.2), custom_call_target="tpu_custom_call" | custom-call | tf_op jit(solution)/shard_map/pallas_call | solution.py:349
  93.8 33.6 %shard_map.38.own = f32[2,128,128]{2,1,0:T(8,128)S(1)} custom-call(f32[15,128,128]{2,1,0:T(8,128)S(1)} %get-tuple-element.9.lead, f32[5,2,128,128]{3,2,1,0:T(8,128)S(1)} %get-tuple-element.10.by_row, f32[5,128,128]{2,1,0:T(8,128)S(1)} %get-tuple-element.11.by_col, f32[2,128,128]{2,1,0:T(8,128)S(1)} %get-tuple-element.12.own), custom_call_target="tpu_custom_call" | custom-call | tf_op jit(solution)/shard_map/pallas_call | solution.py:459
  127.4 24.7 %shard_map.39 = f32[512,1024]{1,0:T(8,128)S(1)} custom-call(f32[2,128,128]{2,1,0:T(8,128)S(1)} %shard_map.38.own), custom_call_target="tpu_custom_call" | custom-call | tf_op jit(solution)/shard_map/pallas_call | solution.py:537
  152.0 1.3 copy.5
Async XLA Ops:
  0.0 1.6 %copy-start = (f32[1,512,1024]{2,1,0:T(8,128)S(1)}, f32[1,512,1024]{2,1,0:T(8,128)}, u32[]{:S(2)}) copy-start(f32[1,512,1024]{2,1,0:T(8,128)} %param.3) | copy-start | bytes 6291460
  1.6 0.9 copy-start.1
  2.5 0.7 copy-start.2

commit v3 on v2

v3 whole, which is shorter than its diff:
```python
import functools

import jax
import jax.numpy as jnp
from jax import lax
from jax.experimental import pallas as pl
from jax.experimental.pallas import tpu as pltpu
from jax.sharding import PartitionSpec as P

BLK = 128
NPAN = 5
STEP = 8
MESH = pl.DeviceIdType.MESH
HIGHEST = lax.Precision.HIGHEST
VMEM = pl.BlockSpec(memory_space=pltpu.VMEM)
PAIRS = [(i, j) for i in range(NPAN) for j in range(i, NPAN)]
NPAIR = len(PAIRS)


def f32(*shape):
    return jax.ShapeDtypeStruct(shape, jnp.float32)


def place():
    grp = lax.axis_index("grp")
    col = lax.axis_index("col")
    return dict(
        g=grp, y=grp // 2, xl=grp % 2, z=lax.axis_index("row"), c=col, xh=col // 2, core=col % 2
    )


def remote(src, dst, send, recv, **where):
    return pltpu.make_async_remote_copy(
        src_ref=src, dst_ref=dst, send_sem=send, recv_sem=recv, device_id=where, device_id_type=MESH
    )


def arrived(dst, send, recv):
    remote(dst, dst, send, recv, grp=lax.axis_index("grp")).wait_recv()


def meet(partners):
    barrier = pltpu.get_barrier_semaphore()
    for where in partners:
        pl.semaphore_signal(barrier, inc=1, device_id=where, device_id_type=MESH)
    pl.semaphore_wait(barrier, len(partners))


def params(ident):
    return pltpu.CompilerParams(collective_id=ident, has_side_effects=True, vmem_limit_bytes=40 << 20)


FAR = (4, 3, 5, 2, 6, 1, 7)
GRP_FAR = (8, 7, 9, 6, 10, 5, 11, 4, 12, 3, 13, 2, 14, 1, 15)
COL_SOURCES = ((0, 0, 0, 2), (0, 1, 2, 2), (1, 0, 4, 1))


def dot(a, b):
    return jnp.dot(a, b, precision=HIGHEST, preferred_element_type=jnp.float32)


def factor_inverse(a):
    row_ids = lax.broadcasted_iota(jnp.int32, (BLK, BLK), 0)
    col_ids = lax.broadcasted_iota(jnp.int32, (BLK, BLK), 1)
    inv = jnp.where(row_ids == col_ids, 1.0, 0.0).astype(jnp.float32)
    done = []
    for start in range(0, BLK, STEP):
        rest = BLK - start
        cols = [jnp.broadcast_to(a[:, start + j : start + j + 1], (rest, BLK)) for j in range(STEP)]
        top_a, top_i = a[:STEP], inv[:STEP]
        rows_a, rows_i = [], []
        for j in range(STEP):
            scale = lax.rsqrt(cols[j][j : j + 1])
            cols[j] = cols[j] * scale
            row_a, row_i = top_a[j : j + 1] * scale, top_i[j : j + 1] * scale
            rows_a.append(row_a)
            rows_i.append(row_i)
            if j + 1 < STEP:
                low = cols[j][:STEP]
                top_a = top_a - low * row_a
                top_i = top_i - low * row_i
                for k in range(j + 1, STEP):
                    cols[k] = cols[k] - cols[j][k : k + 1] * cols[j]
        done.append(jnp.concatenate(rows_i, axis=0))
        if rest > STEP:
            a, inv = a[STEP:], inv[STEP:]
            for j in range(STEP):
                low = cols[j][STEP:]
                a = a - low * rows_a[j]
                inv = inv - low * rows_i[j]
    return jnp.concatenate(done, axis=0)


def dot_nt(a, b):
    return lax.dot_general(
        a, b, (((1,), (1,)), ((), ())), precision=HIGHEST, preferred_element_type=jnp.float32
    )


HOPS = {
    "R1": (0, 1), "R2": (0, 2), "R3": (0, 3), "R4": (0, 4), "L1": (0, -1), "L2": (0, -2), "L3": (0, -3),
    "P0": (1, 0), "RP1": (1, 1), "LP1": (1, -1), "LP2": (1, -2),
    "X2": (1, 2), "X3": (1, 3), "X4": (1, 4), "XL": (1, -3),
}
NAMES = list(HOPS)
ONWARD = {
    "own": (("P0", "x"), ("R1", "r"), ("L1", "l")),
    "P0": (("RP1", "r"), ("LP1", "l")),
    "R1": (("R2", "r"),),
    "L1": (("L2", "l"),),
    "R2": (("R3", "r"), ("X2", "x")),
    "L2": (("L3", "l"),),
    "LP1": (("LP2", "l"),),
    "R3": (("R4", "r"), ("X3", "x")),
    "L3": (("XL", "x"),),
    "R4": (("X4", "x"),),
    "RP1": (), "LP2": (), "X2": (), "XL": (), "X3": (), "X4": (),
}


def whole_kernel(
    mapping, own_t_hbm, normal_hbm, out,
    lead, own, by_row, by_col, own_t, normal, col_t, left, moved, half, mine, parts, lparts, extra, total,
    square, upper, inverse, rows, cols, piece, sem_t,
    sem, send_r, send_l, recv, sx, rx, sy, ry,
    s1, r1, se, re, s2, r2, s3, r3, s4, r4, spx, rr, spy, sc, rcd, sz, rz, sl, rl,
    send6, recv6,
):
    me = place()
    g, y, xl, z, c, core = me["g"], me["y"], me["xl"], me["z"], me["c"], me["core"]
    fetch_t = pltpu.make_async_copy(own_t_hbm, own_t, sem_t)
    fetch_t.start()
    fetch = pltpu.make_async_copy(normal_hbm, normal, sem)
    fetch.start()
    meet(
        [{"grp": (g + d) % 16} for d in range(1, 16)]
        + [{"row": (z + d) % 8} for d in range(1, 8)]
        + [{"col": c ^ 1}, {"col": c ^ 2}]
    )

    fetch_t.wait()

    up, down = (z + 1) % 8, (z + 7) % 8
    reach = 4 - core

    def away_of(slot):
        return (z - (2 * c + slot) + 8) % 8

    def spread(index, src, sends, to):
        return remote(src, col_t.at[index], sends.at[index], recv.at[index], row=to)

    for slot in range(2):
        @pl.when(away_of(slot) == 0)
        def _():
            for part in range(4):
                index = slot * 4 + part
                spread(index, own_t.at[part], send_r, up).start()
                spread(index, own_t.at[part], send_l, down).start()
                col_t[index] = own_t[part]

    fetch.wait()
    for i in range(4):
        block = mapping[0, 4 * z + i] % 4
        turned = dot(own_t[block].T, normal[block])
        for b in range(8):
            left[b, i * BLK : (i + 1) * BLK, :] = turned[:, b * BLK : (b + 1) * BLK]

    rising = (away_of(1) <= reach).astype(jnp.int32)
    for part in range(4):
        for turn in range(2):
            slot = (rising + turn) % 2
            index = slot * 4 + part
            away = away_of(slot)

            @pl.when(away != 0)
            def _():
                arrived(col_t.at[index], send_r.at[index], recv.at[index])

            @pl.when((away > 0) & (away < reach))
            def _():
                spread(index, col_t.at[index], send_r, up).start()

            @pl.when(away > reach + 1)
            def _():
                spread(index, col_t.at[index], send_l, down).start()

    first = (z == 0) & (c == 0)
    order = (4, 1, 7, 2, 6, 3, 5, 0)

    def across(d):
        b = (y + d) % 8
        return remote(
            moved.at[b, pl.ds(2 * (1 - xl), 2)], half.at[b], sx.at[d], rx.at[d], grp=g ^ 1
        )

    def along(d):
        b = (y + d) % 8
        return remote(mine.at[b], parts.at[d], sy.at[d], ry.at[d], grp=(g + 2 * d) % 16)

    for d in order:
        j = (y + d) % 8
        b = j // 4 * 4 + mapping[0, 8 * c + j] % 4
        moved[j] = dot(left[b], col_t[b]).reshape(4, BLK, BLK)

        @pl.when(jnp.logical_not(first))
        def _():
            across(d).start()

    last = PAIRS.index((4, 4))

    @pl.when((z == 1) & (c == 0))
    def _():
        remote(moved.at[4, 0], extra, se, re, row=0).start()

    @pl.when(first)
    def _():
        for t, (i, j) in enumerate(PAIRS):
            if t == last:
                arrived(extra, se, re)
                src = extra
            else:
                src = moved.at[j, i]

            @pl.when(g != t)
            def _():
                remote(src, lparts.at[g], s1.at[t], r1.at[g], grp=t).start()

            @pl.when(g == t)
            def _():
                total[...] = src[...]

    @pl.when(first)
    def _():
        for d in order:
            across(d).start()

    @pl.when(first & (g < NPAIR))
    def _():
        for d in range(1, 16):
            arrived(lparts.at[(g + d) % 16], s1.at[0], r1.at[(g + d) % 16])
        acc = total[...]
        for d in range(1, 16):
            acc = acc + lparts[(g + d) % 16]
        total[...] = acc
        lead[g] = acc
        remote(total, lead.at[g], s2.at[0], r2, col=2).start()
        for d in FAR:
            remote(total, lead.at[g], s2.at[d], r2, row=(z + d) % 8).start()

    def among_members():
        for d in GRP_FAR:
            remote(lead.at[g], lead.at[g], s3.at[d], r3.at[g], grp=(g + d) % 16).start()
        remote(lead.at[g], lead.at[g], s4.at[0], r4.at[g], col=c ^ 1).start()

    @pl.when(first & (g < NPAIR))
    def _():
        among_members()

    for turn, d in enumerate(order):
        b = (y + d) % 8
        across(d).wait_recv()
        mine[b] = moved[b, pl.ds(2 * xl, 2)] + half[b]
        if d:
            along(d).start()
        if turn == 1:
            @pl.when((z != 0) & (c == 0) & (g < NPAIR))
            def _():
                arrived(lead.at[g], s2.at[0], r2)
                among_members()
        if turn == 2:
            @pl.when((z == 0) & (c == 2) & (g < NPAIR))
            def _():
                arrived(lead.at[g], s2.at[0], r2)
                for d2 in FAR:
                    remote(lead.at[g], lead.at[g], s2.at[d2], r2, row=(z + d2) % 8).start()
                among_members()
        if turn == 4:
            @pl.when((z != 0) & (c == 2) & (g < NPAIR))
            def _():
                arrived(lead.at[g], s2.at[0], r2)
                among_members()

    acc = mine[y]
    for d in order[:-1]:
        along(d).wait_recv()
        acc = acc + parts[d]
    own[...] = acc

    for src_z, src_xl, start, count in COL_SOURCES:
        n = src_z * 2 + src_xl
        there = by_col.at[pl.ds(start, count)]
        src = own.at[pl.ds(0, count)]

        @pl.when((z == src_z) & (xl == src_xl))
        def _():
            for d in FAR:
                remote(src, there, sz.at[n, d], rz.at[n], row=(z + d) % 8).start()
            remote(src, there, sl.at[n], rl.at[n], grp=g ^ 1).start()
            by_col[start : start + count] = own[0:count]

    @pl.when((c == 0) & (y < NPAN))
    def _():
        remote(own, by_row.at[y], spx, rr.at[y], col=2).start()
        for d in FAR:
            remote(own, by_row.at[y], spy.at[d], rr.at[y], grp=(g + 2 * d) % 16).start()
        remote(own, by_row.at[y], sc.at[y], rcd.at[y], col=c ^ 1).start()
        by_row[y] = own[...]

    @pl.when(core == 0)
    def _():
        for d in range(1, 16):
            t = (g + d) % 16

            @pl.when(t < NPAIR)
            def _():
                arrived(lead.at[t], s3.at[0], r3.at[t])
                remote(lead.at[t], lead.at[t], s4.at[d], r4.at[t], col=c ^ 1).start()

    @pl.when(core == 1)
    def _():
        for t in range(NPAIR):
            arrived(lead.at[t], s4.at[0], r4.at[t])

    for t, (i, j) in enumerate(PAIRS):
        square[i * BLK : (i + 1) * BLK, j * BLK : (j + 1) * BLK] = lead[t]

    def factor(k):
        low, high = k * BLK, (k + 1) * BLK
        inverse[k] = factor_inverse(square[low:high, low:high])
        if k + 1 < NPAN:
            across_panel = dot(inverse[k], square[low:high, high:])
            upper[low:high, high:] = across_panel
            square[high:, high:] -= dot(across_panel.T, across_panel)

    def rows_to_other_core(sources):
        @pl.when(sources)
        def _():
            for k in range(NPAN):
                @pl.when(y != k)
                def _():
                    arrived(by_row.at[k], spx, rr.at[k])
                    remote(by_row.at[k], by_row.at[k], sc.at[k], rcd.at[k], col=c ^ 1).start()

    factor(0)

    @pl.when((c == 2) & (y < NPAN))
    def _():
        arrived(by_row.at[y], spx, rr.at[y])
        for d in FAR:
            remote(by_row.at[y], by_row.at[y], spy.at[d], rr.at[y], grp=(g + 2 * d) % 16).start()
        remote(by_row.at[y], by_row.at[y], sc.at[y], rcd.at[y], col=c ^ 1).start()

    factor(1)
    factor(2)
    for src_z, src_xl, start, count in COL_SOURCES:
        n = src_z * 2 + src_xl
        there = by_col.at[pl.ds(start, count)]

        @pl.when((z != src_z) & (xl == src_xl))
        def _():
            arrived(there, sz.at[n, 0], rz.at[n])
            remote(there, there, sl.at[n], rl.at[n], grp=g ^ 1).start()

    factor(3)
    rows_to_other_core(c == 0)
    factor(4)
    rows_to_other_core(c == 2)
    for src_z, src_xl, start, count in COL_SOURCES:
        n = src_z * 2 + src_xl

        @pl.when(xl != src_xl)
        def _():
            arrived(by_col.at[pl.ds(start, count)], sl.at[n], rl.at[n])

    @pl.when(core == 1)
    def _():
        for k in range(NPAN):
            arrived(by_row.at[k], sc.at[k], rcd.at[k])

    row_block = 4 * z + 2 * xl
    col_block = 8 * c + y
    which = row_block + lax.broadcasted_iota(jnp.int32, (2 * BLK, BLK), 0) // BLK
    for k in range(NPAN):
        rows[:, k * BLK : (k + 1) * BLK] = by_row[k].reshape(2 * BLK, BLK)
    cols[...] = by_col[...].reshape(NPAN * BLK, BLK)
    panel_piece = jnp.zeros((2 * BLK, BLK), jnp.float32)
    for k in range(NPAN):
        low, high = k * BLK, (k + 1) * BLK
        col_factor = dot(inverse[k], cols[low:high])
        cols[low:high] = col_factor
        row_factor = jnp.where(which >= k, dot_nt(rows[:, low:high], inverse[k]), 0.0)
        rows[:, low:high] = row_factor
        panel_piece = jnp.where(col_block == k, row_factor, panel_piece)
        if k + 1 < NPAN:
            across_panel = upper[low:high, high:]
            cols[high:] -= dot(across_panel.T, col_factor)
            rows[:, high:] -= dot(row_factor, across_panel)
    rest = own[...].reshape(2 * BLK, BLK) - dot(rows[...], cols[...])
    piece[...] = jnp.where(col_block < NPAN, panel_piece, rest).reshape(2, BLK, BLK)

    to = {"x": g ^ 1, "r": (g + 2) % 16, "l": (g + 14) % 16}

    def spot(x, steps, part):
        row = pl.multiple_of((x * 2 + part) * BLK, BLK)
        col = pl.multiple_of(((y - steps + 8) % 8) * BLK, BLK)
        return out.at[pl.ds(row, BLK), pl.ds(col, BLK)]

    def here(name, part):
        other, steps = HOPS[name]
        return spot(1 - xl if other else xl, steps, part)

    def hop(src_name, name, way, part):
        if src_name == "own":
            src, dst = piece.at[part], spot(xl, 0, part)
        else:
            src = dst = here(src_name, part)
        n = NAMES.index(name)
        return remote(src, dst, send6.at[n, part], recv6.at[n, part], grp=to[way])

    for part in range(2):
        for name, way in ONWARD["own"]:
            hop("own", name, way, part).start()
        row = pl.multiple_of((xl * 2 + part) * BLK, BLK)
        out[pl.ds(row, BLK), pl.ds(pl.multiple_of(y * BLK, BLK), BLK)] = piece[part]
    for src_name in list(ONWARD)[1:]:
        for part in range(2):
            n = NAMES.index(src_name)
            arrived(here(src_name, part), send6.at[n, part], recv6.at[n, part])
            for name, way in ONWARD[src_name]:
                hop(src_name, name, way, part).start()
    for src_name in ONWARD:
        for name, way in ONWARD[src_name]:
            for part in range(2):
                hop(src_name, name, way, part).wait_send()

    for slot in range(2):
        away = away_of(slot)
        for part in range(4):
            index = slot * 4 + part

            @pl.when(away < reach)
            def _():
                spread(index, col_t.at[index], send_r, up).wait_send()

            @pl.when((away > reach + 1) | (away == 0))
            def _():
                spread(index, col_t.at[index], send_l, down).wait_send()
    for d in order:
        across(d).wait_send()
        if d:
            along(d).wait_send()

    @pl.when((z == 1) & (c == 0))
    def _():
        remote(extra, extra, se, re, row=0).wait_send()

    @pl.when(first)
    def _():
        for t in range(NPAIR):
            @pl.when(g != t)
            def _():
                remote(extra, lparts.at[g], s1.at[t], r1.at[g], grp=t).wait_send()

        @pl.when(g < NPAIR)
        def _():
            remote(total, lead.at[g], s2.at[0], r2, col=2).wait_send()

    @pl.when((z == 0) & (core == 0) & (g < NPAIR))
    def _():
        for d in FAR:
            remote(total, lead.at[g], s2.at[d], r2, row=(z + d) % 8).wait_send()

    for src_z, src_xl, start, count in COL_SOURCES:
        n = src_z * 2 + src_xl
        there = by_col.at[pl.ds(start, count)]

        @pl.when(xl == src_xl)
        def _():
            @pl.when(z == src_z)
            def _():
                for d in FAR:
                    remote(there, there, sz.at[n, d], rz.at[n], row=(z + d) % 8).wait_send()
            remote(there, there, sl.at[n], rl.at[n], grp=g ^ 1).wait_send()

    @pl.when(core == 0)
    def _():
        @pl.when(y < NPAN)
        def _():
            @pl.when(c == 0)
            def _():
                remote(own, by_row.at[y], spx, rr.at[y], col=2).wait_send()
            for d in FAR:
                remote(own, by_row.at[y], spy.at[d], rr.at[y], grp=(g + 2 * d) % 16).wait_send()
        for k in range(NPAN):
            remote(own, by_row.at[k], sc.at[k], rcd.at[k], col=c ^ 1).wait_send()

        @pl.when(g < NPAIR)
        def _():
            for d in GRP_FAR:
                remote(total, lead.at[g], s3.at[d], r3.at[g], grp=(g + d) % 16).wait_send()
        for d in range(16):
            t = (g + d) % 16

            @pl.when(t < NPAIR)
            def _():
                remote(total, lead.at[t], s4.at[d], r4.at[t], col=c ^ 1).wait_send()


def whole(mapping, own_t, normal):
    dma = pltpu.SemaphoreType.DMA

    def buf(*shape):
        return pltpu.VMEM(shape, jnp.float32)

    order = NPAN * BLK
    hbm = pl.BlockSpec(memory_space=pltpu.HBM)
    return pl.pallas_call(
        whole_kernel,
        out_shape=f32(4 * BLK, 8 * BLK),
        in_specs=[pl.BlockSpec(memory_space=pltpu.SMEM), hbm, hbm],
        out_specs=VMEM,
        scratch_shapes=[
            buf(NPAIR, BLK, BLK), buf(2, BLK, BLK), buf(NPAN, 2, BLK, BLK), buf(NPAN, BLK, BLK),
            buf(4, BLK, BLK), buf(4, BLK, 8 * BLK), buf(8, BLK, BLK), buf(8, 4 * BLK, BLK), buf(8, 4, BLK, BLK),
            buf(8, 2, BLK, BLK), buf(8, 2, BLK, BLK), buf(8, 2, BLK, BLK),
            buf(16, BLK, BLK), buf(BLK, BLK), buf(BLK, BLK),
            buf(order, order), buf(order, order), buf(NPAN, BLK, BLK), buf(2 * BLK, order), buf(order, BLK),
            buf(2, BLK, BLK),
            dma, dma, dma((8,)), dma((8,)), dma((8,)), dma((8,)), dma((8,)), dma((8,)), dma((8,)),
            dma((16,)), dma((16,)), dma, dma, dma((8,)), dma, dma((16,)), dma((16,)), dma((16,)), dma((16,)),
            dma, dma((NPAN,)), dma((8,)), dma((NPAN,)), dma((NPAN,)), dma((3, 8)), dma((3,)), dma((3,)), dma((3,)),
            dma((15, 2)), dma((15, 2)),
        ],
        compiler_params=params(1),
    )(mapping, own_t, normal)


def on_device(normals, transforms, block_map):
    return whole(block_map, transforms[0], normals.reshape(4, BLK, 8 * BLK))


def solution(mesh):
    return jax.shard_map(
        on_device,
        mesh=mesh,
        in_specs=(P("grp", "row", "col"), P("grp", "row", None, None), P("grp", None)),
        out_specs=P("row", "col"),
        check_vma=False,
    )
```

time: 155 us -> 142 us (0.916)
  the two profiles are of different devices: /device:TPU:1 before, /device:TPU:85 now
where the time goes in v3:
time: 142 us
  Pallas kernels  137 us (96%)
  local copies, waits for them, and re-layouts  4.52 us (3%)
    pallas_call x1, Pallas kernels, whole(): pl.pallas_call(whole_kernel, out_shape=f32(4 * BLK, 8 * BLK), in_specs=[p...  137 us
    unnamed x7, local copies, waits for them, and re-layouts  4.52 us

profile of v3, /device:TPU:85, one launch (start us, length us, event | category | flops | bytes accessed | tf_op | source)
XLA Modules:
  0.0 141.7 jit_solution(8733630560303491257)
XLA Ops:
  0.0 0.0 copy-start
  0.0 1.6 %copy-done = f32[1,512,1024]{2,1,0:T(8,128)S(1)} copy-done((f32[1,512,1024]{2,1,0:T(8,128)S(1)}, f32[1,512,1024]{2,1,0:T(8,128)}, u32[]{:S(2)}) %copy-start) | copy-done | bytes 2097176
  1.6 0.0 copy-start.1
  1.6 0.9 copy-done.1
  2.5 0.0 copy-start.2
  2.5 0.7 copy-done.2
  3.2 137.2 %shard_map.37 = f32[512,1024]{1,0:T(8,128)S(1)} custom-call(s32[1,32]{1,0:T(1,128)S(1)} %copy-done.2, f32[4,128,128]{2,1,0:T(8,128)S(1)} %bitcast.3, f32[4,128,1024]{2,1,0:T(8,128)S(1)} %bitcast.2), custom_call_target="tpu_custom_call" | custom-call | tf_op jit(solution)/shard_map/pallas_call | solution.py:517
  140.4 1.3 copy.5
Async XLA Ops:
  0.0 1.6 %copy-start = (f32[1,512,1024]{2,1,0:T(8,128)S(1)}, f32[1,512,1024]{2,1,0:T(8,128)}, u32[]{:S(2)}) copy-start(f32[1,512,1024]{2,1,0:T(8,128)} %param.3) | copy-start | bytes 6291460
  1.6 0.9 copy-start.1
  2.5 0.7 copy-start.2

commit v4 on v3

--- a/solution.py
+++ b/solution.py
@@ -47,7 +47,7 @@
 
 
 def params(ident):
-    return pltpu.CompilerParams(collective_id=ident, has_side_effects=True, vmem_limit_bytes=40 << 20)
+    return pltpu.CompilerParams(collective_id=ident, has_side_effects=True, vmem_limit_bytes=53300000)
 
 
 FAR = (4, 3, 5, 2, 6, 1, 7)
@@ -135,7 +135,8 @@
     meet(
         [{"grp": (g + d) % 16} for d in range(1, 16)]
         + [{"row": (z + d) % 8} for d in range(1, 8)]
-        + [{"col": c ^ 1}, {"col": c ^ 2}]
+        + [{"col": c ^ 1}]
+        + [{"row": (z + d) % 8, "col": c ^ 2} for d in range(8)]
     )
 
     fetch_t.wait()
@@ -197,23 +198,32 @@
         b = (y + d) % 8
         return remote(mine.at[b], parts.at[d], sy.at[d], ry.at[d], grp=(g + 2 * d) % 16)
 
-    for d in order:
-        j = (y + d) % 8
+    def combine(j):
         b = j // 4 * 4 + mapping[0, 8 * c + j] % 4
         moved[j] = dot(left[b], col_t[b]).reshape(4, BLK, BLK)
 
-        @pl.when(jnp.logical_not(first))
-        def _():
+    last = PAIRS.index((4, 4))
+
+    @pl.when(jnp.logical_not(first))
+    def _():
+        @pl.when((z == 1) & (c == 0))
+        def _():
+            combine(4)
+            remote(moved.at[4, 0], extra, se, re, row=0).start()
+
+        for d in order:
+            j = (y + d) % 8
+
+            @pl.when(jnp.logical_not((z == 1) & (c == 0) & (j == 4)))
+            def _():
+                combine(j)
+
             across(d).start()
 
-    last = PAIRS.index((4, 4))
-
-    @pl.when((z == 1) & (c == 0))
-    def _():
-        remote(moved.at[4, 0], extra, se, re, row=0).start()
-
     @pl.when(first)
     def _():
+        for j in range(NPAN):
+            combine(j)
         for t, (i, j) in enumerate(PAIRS):
             if t == last:
                 arrived(extra, se, re)
@@ -229,10 +239,21 @@
             def _():
                 total[...] = src[...]
 
-    @pl.when(first)
-    def _():
+        for j in range(NPAN, 8):
+            combine(j)
         for d in order:
             across(d).start()
+
+    def among_members():
+        for d in GRP_FAR:
+            remote(lead.at[g], lead.at[g], s3.at[d], r3.at[g], grp=(g + d) % 16).start()
+        remote(lead.at[g], lead.at[g], s4.at[0], r4.at[g], col=c ^ 1).start()
+
+    def to_rows(d):
+        return (
+            remote(total, lead.at[g], s2.at[d], r2, row=(z + d) % 8, col=2),
+            remote(total, lead.at[g], s2.at[8 + d], r2, row=(z + d) % 8, col=0),
+        )
 
     @pl.when(first & (g < NPAIR))
     def _():
@@ -243,17 +264,9 @@
             acc = acc + lparts[(g + d) % 16]
         total[...] = acc
         lead[g] = acc
-        remote(total, lead.at[g], s2.at[0], r2, col=2).start()
-        for d in FAR:
-            remote(total, lead.at[g], s2.at[d], r2, row=(z + d) % 8).start()
-
-    def among_members():
-        for d in GRP_FAR:
-            remote(lead.at[g], lead.at[g], s3.at[d], r3.at[g], grp=(g + d) % 16).start()
-        remote(lead.at[g], lead.at[g], s4.at[0], r4.at[g], col=c ^ 1).start()
-
-    @pl.when(first & (g < NPAIR))
-    def _():
+        for d in FAR + (0,):
+            for copy in to_rows(d)[: 2 if d else 1]:
+                copy.start()
         among_members()
 
     for turn, d in enumerate(order):
@@ -262,20 +275,8 @@
         mine[b] = moved[b, pl.ds(2 * xl, 2)] + half[b]
         if d:
             along(d).start()
-        if turn == 1:
-            @pl.when((z != 0) & (c == 0) & (g < NPAIR))
-            def _():
-                arrived(lead.at[g], s2.at[0], r2)
-                among_members()
-        if turn == 2:
-            @pl.when((z == 0) & (c == 2) & (g < NPAIR))
-            def _():
-                arrived(lead.at[g], s2.at[0], r2)
-                for d2 in FAR:
-                    remote(lead.at[g], lead.at[g], s2.at[d2], r2, row=(z + d2) % 8).start()
-                among_members()
-        if turn == 4:
-            @pl.when((z != 0) & (c == 2) & (g < NPAIR))
+        if turn == 5:
+            @pl.when(jnp.logical_not(first) & (core == 0) & (g < NPAIR))
             def _():
                 arrived(lead.at[g], s2.at[0], r2)
                 among_members()
@@ -332,15 +333,6 @@
             upper[low:high, high:] = across_panel
             square[high:, high:] -= dot(across_panel.T, across_panel)
 
-    def rows_to_other_core(sources):
-        @pl.when(sources)
-        def _():
-            for k in range(NPAN):
-                @pl.when(y != k)
-                def _():
-                    arrived(by_row.at[k], spx, rr.at[k])
-                    remote(by_row.at[k], by_row.at[k], sc.at[k], rcd.at[k], col=c ^ 1).start()
-
     factor(0)
 
     @pl.when((c == 2) & (y < NPAN))
@@ -362,9 +354,15 @@
             remote(there, there, sl.at[n], rl.at[n], grp=g ^ 1).start()
 
     factor(3)
-    rows_to_other_core(c == 0)
-    factor(4)
-    rows_to_other_core(c == 2)
+
+    @pl.when(core == 0)
+    def _():
+        for k in range(NPAN):
+            @pl.when(y != k)
+            def _():
+                arrived(by_row.at[k], spx, rr.at[k])
+                remote(by_row.at[k], by_row.at[k], sc.at[k], rcd.at[k], col=c ^ 1).start()
+
     for src_z, src_xl, start, count in COL_SOURCES:
         n = src_z * 2 + src_xl
 
@@ -384,18 +382,18 @@
         rows[:, k * BLK : (k + 1) * BLK] = by_row[k].reshape(2 * BLK, BLK)
     cols[...] = by_col[...].reshape(NPAN * BLK, BLK)
     panel_piece = jnp.zeros((2 * BLK, BLK), jnp.float32)
+    rest = own[...].reshape(2 * BLK, BLK)
+    factor(4)
     for k in range(NPAN):
         low, high = k * BLK, (k + 1) * BLK
         col_factor = dot(inverse[k], cols[low:high])
-        cols[low:high] = col_factor
         row_factor = jnp.where(which >= k, dot_nt(rows[:, low:high], inverse[k]), 0.0)
-        rows[:, low:high] = row_factor
         panel_piece = jnp.where(col_block == k, row_factor, panel_piece)
         if k + 1 < NPAN:
             across_panel = upper[low:high, high:]
             cols[high:] -= dot(across_panel.T, col_factor)
             rows[:, high:] -= dot(row_factor, across_panel)
-    rest = own[...].reshape(2 * BLK, BLK) - dot(rows[...], cols[...])
+        rest = rest - dot(row_factor, col_factor)
     piece[...] = jnp.where(col_block < NPAN, panel_piece, rest).reshape(2, BLK, BLK)
 
     to = {"x": g ^ 1, "r": (g + 2) % 16, "l": (g + 14) % 16}
@@ -463,12 +461,9 @@
 
         @pl.when(g < NPAIR)
         def _():
-            remote(total, lead.at[g], s2.at[0], r2, col=2).wait_send()
-
-    @pl.when((z == 0) & (core == 0) & (g < NPAIR))
-    def _():
-        for d in FAR:
-            remote(total, lead.at[g], s2.at[d], r2, row=(z + d) % 8).wait_send()
+            for d in FAR + (0,):
+                for copy in to_rows(d)[: 2 if d else 1]:
+                    copy.wait_send()
 
     for src_z, src_xl, start, count in COL_SOURCES:
         n = src_z * 2 + src_xl
@@ -527,7 +522,7 @@
             buf(order, order), buf(order, order), buf(NPAN, BLK, BLK), buf(2 * BLK, order), buf(order, BLK),
             buf(2, BLK, BLK),
             dma, dma, dma((8,)), dma((8,)), dma((8,)), dma((8,)), dma((8,)), dma((8,)), dma((8,)),
-            dma((16,)), dma((16,)), dma, dma, dma((8,)), dma, dma((16,)), dma((16,)), dma((16,)), dma((16,)),
+            dma((16,)), dma((16,)), dma, dma, dma((16,)), dma, dma((16,)), dma((16,)), dma((16,)), dma((16,)),
             dma, dma((NPAN,)), dma((8,)), dma((NPAN,)), dma((NPAN,)), dma((3, 8)), dma((3,)), dma((3,)), dma((3,)),
             dma((15, 2)), dma((15, 2)),
         ],

time: 142 us -> 133 us (0.937)
  the two profiles are of different devices: /device:TPU:85 before, /device:TPU:5 now
where the time goes in v4:
time: 133 us
  Pallas kernels  130 us (98%)
  local copies, waits for them, and re-layouts  2.93 us (2%)
    pallas_call x1, Pallas kernels, whole(): pl.pallas_call(whole_kernel, out_shape=f32(4 * BLK, 8 * BLK), in_specs=[p...  130 us
    unnamed x5, local copies, waits for them, and re-layouts  2.93 us

profile of v4, /device:TPU:5, one launch (start us, length us, event | category | flops | bytes accessed | tf_op | source)
XLA Modules:
  0.0 132.7 jit_solution(6822124237790981743)
XLA Ops:
  0.0 0.0 copy-start
  0.0 0.9 copy-done
  1.0 0.0 copy-start.1
  1.0 0.7 copy-done.1
  1.6 129.8 %shard_map.37 = f32[512,1024]{1,0:T(8,128)S(1)} custom-call(s32[1,32]{1,0:T(1,128)S(1)} %copy-done.1, f32[4,128,128]{2,1,0:T(8,128)S(1)} %bitcast.2, f32[4,128,1024]{2,1,0:T(8,128)} %bitcast.3), custom_call_target="tpu_custom_call" | custom-call | tf_op jit(solution)/shard_map/pallas_call | solution.py:512
  131.4 1.3 copy.5
Async XLA Ops:
  0.0 0.9 copy-start
  1.0 0.7 copy-start.1

commit v5 on v4

--- a/solution.py
+++ b/solution.py
@@ -62,33 +62,30 @@
 def factor_inverse(a):
     row_ids = lax.broadcasted_iota(jnp.int32, (BLK, BLK), 0)
     col_ids = lax.broadcasted_iota(jnp.int32, (BLK, BLK), 1)
-    inv = jnp.where(row_ids == col_ids, 1.0, 0.0).astype(jnp.float32)
     done = []
     for start in range(0, BLK, STEP):
         rest = BLK - start
         cols = [jnp.broadcast_to(a[:, start + j : start + j + 1], (rest, BLK)) for j in range(STEP)]
-        top_a, top_i = a[:STEP], inv[:STEP]
-        rows_a, rows_i = [], []
+        here = (col_ids[start:] >= start) & (col_ids[start:] < start + STEP)
+        unit = jnp.where(col_ids[start:] == row_ids[start:], 1.0, 0.0).astype(jnp.float32)
+        a = jnp.where(here, unit, a)
+        top = a[:STEP]
+        rows = []
         for j in range(STEP):
             scale = lax.rsqrt(cols[j][j : j + 1])
             cols[j] = cols[j] * scale
-            row_a, row_i = top_a[j : j + 1] * scale, top_i[j : j + 1] * scale
-            rows_a.append(row_a)
-            rows_i.append(row_i)
+            row = top[j : j + 1] * scale
+            rows.append(row)
             if j + 1 < STEP:
-                low = cols[j][:STEP]
-                top_a = top_a - low * row_a
-                top_i = top_i - low * row_i
+                top = top - cols[j][:STEP] * row
                 for k in range(j + 1, STEP):
                     cols[k] = cols[k] - cols[j][k : k + 1] * cols[j]
-        done.append(jnp.concatenate(rows_i, axis=0))
+        done.append(jnp.concatenate(rows, axis=0))
         if rest > STEP:
-            a, inv = a[STEP:], inv[STEP:]
+            a = a[STEP:]
             for j in range(STEP):
-                low = cols[j][STEP:]
-                a = a - low * rows_a[j]
-                inv = inv - low * rows_i[j]
-    return jnp.concatenate(done, axis=0)
+                a = a - cols[j][STEP:] * rows[j]
+    return jnp.where(col_ids <= row_ids, jnp.concatenate(done, axis=0), 0.0)
 
 
 def dot_nt(a, b):
@@ -120,11 +117,11 @@
 
 def whole_kernel(
     mapping, own_t_hbm, normal_hbm, out,
-    lead, own, by_row, by_col, own_t, normal, col_t, left, moved, half, mine, parts, lparts, extra, total,
+    lead, own, by_row, by_col, own_t, normal, col_t, left, moved, half, mine, parts, lparts, lblk, lx, lsum, total,
     square, upper, inverse, rows, cols, piece, sem_t,
     sem, send_r, send_l, recv, sx, rx, sy, ry,
     s1, r1, se, re, s2, r2, s3, r3, s4, r4, spx, rr, spy, sc, rcd, sz, rz, sl, rl,
-    send6, recv6,
+    send6, recv6, sl1, rl1,
 ):
     me = place()
     g, y, xl, z, c, core = me["g"], me["y"], me["xl"], me["z"], me["c"], me["core"]
@@ -209,7 +206,7 @@
         @pl.when((z == 1) & (c == 0))
         def _():
             combine(4)
-            remote(moved.at[4, 0], extra, se, re, row=0).start()
+            remote(moved.at[4, 0], lblk.at[last], se, re, row=0).start()
 
         for d in order:
             j = (y + d) % 8
@@ -224,20 +221,34 @@
     def _():
         for j in range(NPAN):
             combine(j)
-        for t, (i, j) in enumerate(PAIRS):
-            if t == last:
-                arrived(extra, se, re)
-                src = extra
-            else:
-                src = moved.at[j, i]
-
-            @pl.when(g != t)
-            def _():
-                remote(src, lparts.at[g], s1.at[t], r1.at[g], grp=t).start()
-
-            @pl.when(g == t)
-            def _():
-                total[...] = src[...]
+        for t, (i, j) in enumerate(PAIRS[:last]):
+            lblk[t] = moved[j, i]
+        for d in order:
+            k = (y + d) % 8
+            t = 2 * k + 1 - xl
+
+            @pl.when(t == last)
+            def _():
+                arrived(lblk.at[last], se, re)
+
+            @pl.when(t < NPAIR)
+            def _():
+                remote(lblk.at[t], lx.at[k], sl1.at[k], rl1.at[k], grp=g ^ 1).start()
+
+        for d in order:
+            k = (y + d) % 8
+            t = 2 * k + xl
+
+            @pl.when(t == last)
+            def _():
+                arrived(lblk.at[last], se, re)
+
+            @pl.when(t < NPAIR)
+            def _():
+                arrived(lx.at[k], sl1.at[k], rl1.at[k])
+                lsum[k] = lblk[t] + lx[k]
+                if d:
+                    remote(lsum.at[k], lparts.at[d], s1.at[d], r1.at[d], grp=(g + 2 * d) % 16).start()
 
         for j in range(NPAN, 8):
             combine(j)
@@ -257,18 +268,17 @@
 
     @pl.when(first & (g < NPAIR))
     def _():
-        for d in range(1, 16):
-            arrived(lparts.at[(g + d) % 16], s1.at[0], r1.at[(g + d) % 16])
-        acc = total[...]
-        for d in range(1, 16):
-            acc = acc + lparts[(g + d) % 16]
+        acc = lsum[y]
+        for d in order[:-1]:
+            arrived(lparts.at[d], s1.at[d], r1.at[d])
+            acc = acc + lparts[d]
         total[...] = acc
         lead[g] = acc
         for d in FAR + (0,):
             for copy in to_rows(d)[: 2 if d else 1]:
                 copy.start()
-        among_members()
-
+
+    late = first | ((c == 2) & (z < 3))
     for turn, d in enumerate(order):
         b = (y + d) % 8
         across(d).wait_recv()
@@ -276,10 +286,18 @@
         if d:
             along(d).start()
         if turn == 5:
-            @pl.when(jnp.logical_not(first) & (core == 0) & (g < NPAIR))
+            @pl.when((core == 0) & (g < NPAIR) & jnp.logical_not(late))
             def _():
                 arrived(lead.at[g], s2.at[0], r2)
                 among_members()
+
+    @pl.when((core == 0) & (g < NPAIR) & late)
+    def _():
+        @pl.when(jnp.logical_not(first))
+        def _():
+            arrived(lead.at[g], s2.at[0], r2)
+
+        among_members()
 
     acc = mine[y]
     for d in order[:-1]:
@@ -309,13 +327,13 @@
 
     @pl.when(core == 0)
     def _():
-        for d in range(1, 16):
-            t = (g + d) % 16
+        for d in GRP_FAR:
+            t = (g + 16 - d) % 16
 
             @pl.when(t < NPAIR)
             def _():
                 arrived(lead.at[t], s3.at[0], r3.at[t])
-                remote(lead.at[t], lead.at[t], s4.at[d], r4.at[t], col=c ^ 1).start()
+                remote(lead.at[t], lead.at[t], s4.at[16 - d], r4.at[t], col=c ^ 1).start()
 
     @pl.when(core == 1)
     def _():
@@ -450,14 +468,21 @@
 
     @pl.when((z == 1) & (c == 0))
     def _():
-        remote(extra, extra, se, re, row=0).wait_send()
+        remote(total, total, se, re, row=0).wait_send()
 
     @pl.when(first)
     def _():
-        for t in range(NPAIR):
-            @pl.when(g != t)
-            def _():
-                remote(extra, lparts.at[g], s1.at[t], r1.at[g], grp=t).wait_send()
+        for d in order:
+            k = (y + d) % 8
+
+            @pl.when(2 * k + 1 - xl < NPAIR)
+            def _():
+                remote(total, total, sl1.at[k], rl1.at[k], grp=g ^ 1).wait_send()
+
+            if d:
+                @pl.when(2 * k + xl < NPAIR)
+                def _():
+                    remote(total, total, s1.at[d], r1.at[d], grp=g ^ 1).wait_send()
 
         @pl.when(g < NPAIR)
         def _():
@@ -518,13 +543,13 @@
             buf(NPAIR, BLK, BLK), buf(2, BLK, BLK), buf(NPAN, 2, BLK, BLK), buf(NPAN, BLK, BLK),
             buf(4, BLK, BLK), buf(4, BLK, 8 * BLK), buf(8, BLK, BLK), buf(8, 4 * BLK, BLK), buf(8, 4, BLK, BLK),
             buf(8, 2, BLK, BLK), buf(8, 2, BLK, BLK), buf(8, 2, BLK, BLK),
-            buf(16, BLK, BLK), buf(BLK, BLK), buf(BLK, BLK),
+            buf(8, BLK, BLK), buf(NPAIR, BLK, BLK), buf(8, BLK, BLK), buf(8, BLK, BLK), buf(BLK, BLK),
             buf(order, order), buf(order, order), buf(NPAN, BLK, BLK), buf(2 * BLK, order), buf(order, BLK),
             buf(2, BLK, BLK),
             dma, dma, dma((8,)), dma((8,)), dma((8,)), dma((8,)), dma((8,)), dma((8,)), dma((8,)),
             dma((16,)), dma((16,)), dma, dma, dma((16,)), dma, dma((16,)), dma((16,)), dma((16,)), dma((16,)),
             dma, dma((NPAN,)), dma((8,)), dma((NPAN,)), dma((NPAN,)), dma((3, 8)), dma((3,)), dma((3,)), dma((3,)),
-            dma((15, 2)), dma((15, 2)),
+            dma((15, 2)), dma((15, 2)), dma((8,)), dma((8,)),
         ],
         compiler_params=params(1),
     )(mapping, own_t, normal)

time: 133 us -> 133 us (level)
  the two profiles are of different devices: /device:TPU:5 before, /device:TPU:1 now
where the time goes in v5:
time: 133 us
  Pallas kernels  130 us (98%)
  local copies, waits for them, and re-layouts  2.93 us (2%)
    pallas_call x1, Pallas kernels, whole(): pl.pallas_call(whole_kernel, out_shape=f32(4 * BLK, 8 * BLK), in_specs=[p...  130 us
    unnamed x5, local copies, waits for them, and re-layouts  2.93 us

profile of v5, /device:TPU:1, one launch (start us, length us, event | category | flops | bytes accessed | tf_op | source)
XLA Modules:
  0.0 132.6 jit_solution(1503361863650706644)
XLA Ops:
  0.0 0.0 copy-start
  0.0 0.9 copy-done
  1.0 0.0 copy-start.1
  1.0 0.7 copy-done.1
  1.6 129.6 %shard_map.37 = f32[512,1024]{1,0:T(8,128)S(1)} custom-call(s32[1,32]{1,0:T(1,128)S(1)} %copy-done.1, f32[4,128,128]{2,1,0:T(8,128)S(1)} %bitcast.2, f32[4,128,1024]{2,1,0:T(8,128)} %bitcast.3), custom_call_target="tpu_custom_call" | custom-call | tf_op jit(solution)/shard_map/pallas_call | solution.py:537
  131.2 1.3 copy.5
Async XLA Ops:
  0.0 0.9 copy-start
  1.0 0.7 copy-start.1

commit v6 on v5

--- a/solution.py
+++ b/solution.py
@@ -10,6 +10,7 @@
 BLK = 128
 NPAN = 5
 STEP = 8
+HALF = 64
 MESH = pl.DeviceIdType.MESH
 HIGHEST = lax.Precision.HIGHEST
 VMEM = pl.BlockSpec(memory_space=pltpu.VMEM)
@@ -121,7 +122,7 @@
     square, upper, inverse, rows, cols, piece, sem_t,
     sem, send_r, send_l, recv, sx, rx, sy, ry,
     s1, r1, se, re, s2, r2, s3, r3, s4, r4, spx, rr, spy, sc, rcd, sz, rz, sl, rl,
-    send6, recv6, sl1, rl1,
+    send6, recv6, sl1, rl1, s5,
 ):
     me = place()
     g, y, xl, z, c, core = me["g"], me["y"], me["xl"], me["z"], me["c"], me["core"]
@@ -255,9 +256,17 @@
         for d in order:
             across(d).start()
 
+    def to_members():
+        for d in GRP_FAR:
+            copy = remote(lead.at[g], lead.at[g], s3.at[d], r3.at[g], grp=(g + d) % 16)
+            yield (((g + d) % 16) // 2 - y + 8) % 8 != 4, copy
+
     def among_members():
-        for d in GRP_FAR:
-            remote(lead.at[g], lead.at[g], s3.at[d], r3.at[g], grp=(g + d) % 16).start()
+        for near, copy in to_members():
+            @pl.when(near)
+            def _():
+                copy.start()
+
         remote(lead.at[g], lead.at[g], s4.at[0], r4.at[g], col=c ^ 1).start()
 
     def to_rows(d):
@@ -278,7 +287,7 @@
             for copy in to_rows(d)[: 2 if d else 1]:
                 copy.start()
 
-    late = first | ((c == 2) & (z < 3))
+    late = (c == 2) & (z < 3)
     for turn, d in enumerate(order):
         b = (y + d) % 8
         across(d).wait_recv()
@@ -288,15 +297,15 @@
         if turn == 5:
             @pl.when((core == 0) & (g < NPAIR) & jnp.logical_not(late))
             def _():
-                arrived(lead.at[g], s2.at[0], r2)
+                @pl.when(jnp.logical_not(first))
+                def _():
+                    arrived(lead.at[g], s2.at[0], r2)
+
                 among_members()
 
     @pl.when((core == 0) & (g < NPAIR) & late)
     def _():
-        @pl.when(jnp.logical_not(first))
-        def _():
-            arrived(lead.at[g], s2.at[0], r2)
-
+        arrived(lead.at[g], s2.at[0], r2)
         among_members()
 
     acc = mine[y]
@@ -325,12 +334,24 @@
         remote(own, by_row.at[y], sc.at[y], rcd.at[y], col=c ^ 1).start()
         by_row[y] = own[...]
 
+    def passed(t, q):
+        return remote(lead.at[t], lead.at[t], s5.at[q], r3.at[t], grp=(g + 14) % 16)
+
     @pl.when(core == 0)
     def _():
+        for q in range(2):
+            t = (y + 3) % 8 * 2 + q
+
+            @pl.when(t < NPAIR)
+            def _():
+                arrived(lead.at[t], s3.at[0], r3.at[t])
+                passed(t, q).start()
+                remote(lead.at[t], lead.at[t], s4.at[(t - g + 16) % 16], r4.at[t], col=c ^ 1).start()
+
         for d in GRP_FAR:
             t = (g + 16 - d) % 16
 
-            @pl.when(t < NPAIR)
+            @pl.when((t < NPAIR) & (t // 2 != (y + 3) % 8))
             def _():
                 arrived(lead.at[t], s3.at[0], r3.at[t])
                 remote(lead.at[t], lead.at[t], s4.at[16 - d], r4.at[t], col=c ^ 1).start()
@@ -412,14 +433,14 @@
             cols[high:] -= dot(across_panel.T, col_factor)
             rows[:, high:] -= dot(row_factor, across_panel)
         rest = rest - dot(row_factor, col_factor)
-    piece[...] = jnp.where(col_block < NPAN, panel_piece, rest).reshape(2, BLK, BLK)
+    piece[...] = jnp.where(col_block < NPAN, panel_piece, rest).reshape(4, HALF, BLK)
 
     to = {"x": g ^ 1, "r": (g + 2) % 16, "l": (g + 14) % 16}
 
     def spot(x, steps, part):
-        row = pl.multiple_of((x * 2 + part) * BLK, BLK)
+        row = pl.multiple_of((x * 4 + part) * HALF, HALF)
         col = pl.multiple_of(((y - steps + 8) % 8) * BLK, BLK)
-        return out.at[pl.ds(row, BLK), pl.ds(col, BLK)]
+        return out.at[pl.ds(row, HALF), pl.ds(col, BLK)]
 
     def here(name, part):
         other, steps = HOPS[name]
@@ -433,20 +454,20 @@
         n = NAMES.index(name)
         return remote(src, dst, send6.at[n, part], recv6.at[n, part], grp=to[way])
 
-    for part in range(2):
+    for part in range(4):
         for name, way in ONWARD["own"]:
             hop("own", name, way, part).start()
-        row = pl.multiple_of((xl * 2 + part) * BLK, BLK)
-        out[pl.ds(row, BLK), pl.ds(pl.multiple_of(y * BLK, BLK), BLK)] = piece[part]
+        row = pl.multiple_of((xl * 4 + part) * HALF, HALF)
+        out[pl.ds(row, HALF), pl.ds(pl.multiple_of(y * BLK, BLK), BLK)] = piece[part]
     for src_name in list(ONWARD)[1:]:
-        for part in range(2):
+        for part in range(4):
             n = NAMES.index(src_name)
             arrived(here(src_name, part), send6.at[n, part], recv6.at[n, part])
             for name, way in ONWARD[src_name]:
                 hop(src_name, name, way, part).start()
     for src_name in ONWARD:
         for name, way in ONWARD[src_name]:
-            for part in range(2):
+            for part in range(4):
                 hop(src_name, name, way, part).wait_send()
 
     for slot in range(2):
@@ -516,8 +537,18 @@
 
         @pl.when(g < NPAIR)
         def _():
-            for d in GRP_FAR:
-                remote(total, lead.at[g], s3.at[d], r3.at[g], grp=(g + d) % 16).wait_send()
+            for near, copy in to_members():
+                @pl.when(near)
+                def _():
+                    copy.wait_send()
+
+        for q in range(2):
+            t = (y + 3) % 8 * 2 + q
+
+            @pl.when(t < NPAIR)
+            def _():
+                passed(t, q).wait_send()
+
         for d in range(16):
             t = (g + d) % 16
 
@@ -545,11 +576,11 @@
             buf(8, 2, BLK, BLK), buf(8, 2, BLK, BLK), buf(8, 2, BLK, BLK),
             buf(8, BLK, BLK), buf(NPAIR, BLK, BLK), buf(8, BLK, BLK), buf(8, BLK, BLK), buf(BLK, BLK),
             buf(order, order), buf(order, order), buf(NPAN, BLK, BLK), buf(2 * BLK, order), buf(order, BLK),
-            buf(2, BLK, BLK),
+            buf(4, HALF, BLK),
             dma, dma, dma((8,)), dma((8,)), dma((8,)), dma((8,)), dma((8,)), dma((8,)), dma((8,)),
             dma((16,)), dma((16,)), dma, dma, dma((16,)), dma, dma((16,)), dma((16,)), dma((16,)), dma((16,)),
             dma, dma((NPAN,)), dma((8,)), dma((NPAN,)), dma((NPAN,)), dma((3, 8)), dma((3,)), dma((3,)), dma((3,)),
-            dma((15, 2)), dma((15, 2)), dma((8,)), dma((8,)),
+            dma((15, 4)), dma((15, 4)), dma((8,)), dma((8,)), dma((2,)),
         ],
         compiler_params=params(1),
     )(mapping, own_t, normal)

time: 133 us -> 142 us (1.068)
  Pallas kernels: 130 us -> 138 us
    pallas_call x1, Pallas kernels: 130 us -> 138 us  [whole(): pl.pallas_call(whole_kernel, out_shape=f32(4 * BLK, 8 * BLK), in_specs=[p...]
where the time goes in v6:
time: 142 us; the launch traced here: 141 us
  Pallas kernels  138 us (97%)
  local copies, waits for them, and re-layouts  2.93 us (2%)
    pallas_call x1, Pallas kernels, whole(): pl.pallas_call(whole_kernel, out_shape=f32(4 * BLK, 8 * BLK), in_specs=[p...  138 us
    unnamed x5, local copies, waits for them, and re-layouts  2.93 us

profile of v6, /device:TPU:1, one launch (start us, length us, event | category | flops | bytes accessed | tf_op | source)
XLA Modules:
  0.0 141.4 jit_solution(13357558483111272538)
XLA Ops:
  0.0 0.0 copy-start
  0.0 0.9 copy-done
  1.0 0.0 copy-start.1
  1.0 0.7 copy-done.1
  1.6 138.4 %shard_map.37 = f32[512,1024]{1,0:T(8,128)S(1)} custom-call(s32[1,32]{1,0:T(1,128)S(1)} %copy-done.1, f32[4,128,128]{2,1,0:T(8,128)S(1)} %bitcast.2, f32[4,128,1024]{2,1,0:T(8,128)} %bitcast.3), custom_call_target="tpu_custom_call" | custom-call | tf_op jit(solution)/shard_map/pallas_call | solution.py:568
  140.0 1.3 copy.5
Async XLA Ops:
  0.0 0.9 copy-start
  1.0 0.7 copy-start.1
